TPU v7x, 128 devices: a whole 4x4x4 slice. The times are simulated.
128 devices in a mesh: gx: 4 (over x), gy: 4 (over y), gz: 8 (over z, core).
Axes of the slice: x: 4, y: 4, z: 4, core: 2. Of those that a mesh axis runs over, the one named last changes fastest.
Arguments:
- right_side: float32 [5, 2048, 8, 128], P(None, ('gx', 'gy', 'gz')), may hold values from -6 to 6
- diag_inverse: bfloat16 [5, 2048, 128, 128], P(None, ('gx', 'gy', 'gz')), may hold values from -0.5 to 0.5
- off_blocks: bfloat16 [4, 16384, 128, 128], P(None, ('gx', 'gy', 'gz')), may hold values from -0.375 to 0.375
- live_counts: int32 [5, 128], P(None, ('gx', 'gy', 'gz')), may hold values from 1 to 16, as said below
- source_slot: int32 [4, 16384], P(None, ('gx', 'gy', 'gz')), may hold values from 0 to 15, as said below
- target_owner: int32 [4, 16384], P(None, ('gx', 'gy', 'gz')), may hold values from 0 to 127, as said below
- target_block: int32 [4, 16384], P(None, ('gx', 'gy', 'gz')), may hold values from 16 to 79, as said below
Outputs:
- solution: float32 [5, 2048, 8, 128], P(None, ('gx', 'gy', 'gz'))
Inputs may be any that keep to these rules, and one draw needn't show every extreme that they name: `live_counts`: slots at or past a device's count in a level are empty; in every level some device has all 16 slots live. `source_slot`: names a live slot of the issuing device in the same level. `target_owner`: in every level, each device's records go exactly 2 each to 64 distinct owners and none to the others. `target_block`: the level part is later than the record's own level, and the slot is live at the owner in that level.
All inputs are finite; a program needn't handle non-finite values.
Results may differ from a plain program's by a relative error of at most 0.013.
Values sent between devices are 32-bit elements; how exact they have to be, the bound alone decides.
No kernel may reach another device: no remote copies, remote signals or barrier semaphores. Data moves between devices by JAX's collectives and lax.ppermute only.
A program may use at most 64 MiB of HBM per device.

v0:
```python
import jax
import jax.numpy as jnp
from jax import lax
from jax.sharding import PartitionSpec as P

CAP = 2


def split_up(x, dim, devices):
    lengths = x.shape
    pieces = x.reshape(*lengths[:dim], devices, lengths[dim] // devices, *lengths[dim + 1 :])
    return jnp.moveaxis(pieces, dim, 0)


def laid_out(pieces, dim):
    lengths = list(pieces.shape[1:])
    lengths[dim] *= pieces.shape[0]
    return jnp.moveaxis(pieces, 0, dim).reshape(lengths)


def one_exchange(x, axis, axes, splits, concats):
    sizes = [lax.axis_size(a) for a in axes]
    pieces = split_up(x, splits[0], sizes[0])
    pieces = jnp.moveaxis(split_up(pieces, splits[1] + 1, sizes[1]), 0, 1)
    inside = pieces.shape[2:]
    pieces = pieces.reshape(-1, *inside)
    pieces = lax.all_to_all(pieces, axis, split_axis=0, concat_axis=0, tiled=True)
    pieces = laid_out(pieces.reshape(*sizes, *inside), concats[0] + 1)
    return laid_out(pieces, concats[1])


def shards(
    right_side, diag_inverse, off_blocks, live_counts, source_slot, target_owner, target_block
):
    levels_total = right_side.shape[0]
    slots = right_side.shape[1]
    rhs_count = right_side.shape[2]
    width = right_side.shape[3]
    flat_width = rhs_count * width
    records = off_blocks.shape[1]
    owners = lax.axis_size(("gx", "gy", "gz"))
    slot_ids = jnp.arange(slots, dtype=jnp.int32)
    owner_ids = jnp.arange(owners, dtype=jnp.int32)
    buffer_ids = jnp.arange(owners * CAP, dtype=jnp.int32)
    block_ids = jnp.arange(levels_total * slots, dtype=jnp.int32)
    accumulated = jnp.zeros((levels_total * slots, flat_width), jnp.float32)
    results = []
    for level_at in range(levels_total):
        pending = accumulated[level_at * slots : (level_at + 1) * slots].reshape(
            slots, rhs_count, width
        )
        work_rows = (right_side[level_at] - pending).astype(jnp.bfloat16)
        solved = jnp.einsum(
            "srb,sbc->src", work_rows, diag_inverse[level_at], preferred_element_type=jnp.float32
        )
        solved = jnp.where(
            (slot_ids < live_counts[level_at, 0])[:, None, None], solved, jnp.float32(0.0)
        )
        results.append(solved)
        if level_at + 1 < levels_total:
            rounded = solved.astype(jnp.bfloat16)
            picker = (source_slot[level_at][:, None] == slot_ids[None, :]).astype(jnp.bfloat16)
            picked = jnp.einsum(
                "ks,srb->krb", picker, rounded, preferred_element_type=jnp.float32
            ).astype(jnp.bfloat16)
            contribution = jnp.einsum(
                "krb,kbc->krc", picked, off_blocks[level_at], preferred_element_type=jnp.float32
            )
            contribution = contribution.reshape(records, flat_width)
            owners_now = target_owner[level_at]
            blocks_now = target_block[level_at]
            owner_hits = (owners_now[:, None] == owner_ids[None, :]).astype(jnp.int32)
            position = jnp.sum(jnp.cumsum(owner_hits, axis=0) * owner_hits, axis=1) - 1
            slot_of = owners_now * CAP + position
            packer = buffer_ids[:, None] == slot_of[None, :]
            outgoing = jnp.dot(
                packer.astype(jnp.float32), contribution, precision=lax.Precision.HIGHEST
            )
            labels = jnp.sum(packer.astype(jnp.int32) * (blocks_now + 1)[None, :], axis=1) - 1
            across = lax.axis_size(("gx", "gy"))
            along = lax.axis_size("gz")
            arrived, received_labels = (
                one_exchange(
                    outgoing.reshape(across, along, CAP, flat_width),
                    ("gx", "gy", "gz"),
                    (("gx", "gy"), "gz"),
                    (0, 1),
                    (0, 1),
                ),
                one_exchange(
                    labels.reshape(across, along, CAP),
                    ("gx", "gy", "gz"),
                    (("gx", "gy"), "gz"),
                    (0, 1),
                    (0, 1),
                ),
            )
            arrived = arrived.reshape(owners * CAP, flat_width)
            received_labels = received_labels.reshape(owners * CAP)
            placer = (block_ids[:, None] == received_labels[None, :]).astype(jnp.float32)
            accumulated = accumulated + jnp.dot(placer, arrived, precision=lax.Precision.HIGHEST)
    return jnp.stack(results)


def solution(mesh):
    in_specs = (
        P(None, ("gx", "gy", "gz"), None, None),
        P(None, ("gx", "gy", "gz"), None, None),
        P(None, ("gx", "gy", "gz"), None, None),
        P(None, ("gx", "gy", "gz")),
        P(None, ("gx", "gy", "gz")),
        P(None, ("gx", "gy", "gz")),
        P(None, ("gx", "gy", "gz")),
    )
    out_specs = P(None, ("gx", "gy", "gz"), None, None)
    return jax.shard_map(shards, mesh=mesh, in_specs=in_specs, out_specs=out_specs, check_vma=False)
```

profile of v0, /device:TPU:1, one launch (start us, length us, event | category | flops | bytes accessed | tf_op | source)
XLA Modules:
  0.0 187.4 jit_solution(17708608084663350231)
XLA Ops:
  0.0 0.7 slice_bitcast_fusion.7
  1.1 0.8 fusion.73
  2.9 0.8 add_bitcast_fusion
  3.9 0.8 fusion.74
  4.9 0.8 sub.55
  5.7 11.5 %all-to-all-start = ((s32[128,1,1,2]{3,2,1,0:T(1,128)}), s32[128,1,1,2]{3,2,1,0:T(1,128)S(1)}, u32[]{:S(2)}, u32[]{:S(2)}) async-start(s32[128,1,1,2]{3,2,1,0:T(1,128)} %bitcast.10), calls=%async_computation | async-start | bytes 131072 | tf_op jit(solution)/shard_map/all_to_all | solution.py:27
  17.2 1.5 fusion.77
  18.7 0.6 iota_compare_fusion.24
  19.3 0.8 slice_bitcast_fusion.3
  20.1 1.3 bitcast_dynamic-update-slice_fusion.3
  21.7 3.4 %fusion.6 = f32[128,8,128]{2,1,0:T(8,128)S(1)} fusion(bf16[4,128,128,128]{3,2,1,0:T(8,128)(2,1)} %param.9, bf16[128,8,128]{2,0,1:T(8,128)(2,1)S(1)} %convolution_convert_fusion.3), kind=kOutput, calls=%fused_computation.6 | convolution fusion | flops 33554432 | bytes 4980736 | tf_op jit(solution)/shard_map/krb,kbc->krc/dot_general | solution.py:66
  25.9 1.8 copy.31
  27.7 9.8 %all-to-all-start.1 = ((f32[128,1,1,2,1024]{4,3,2,1,0:T(2,128)}), f32[128,1,1,2,1024]{4,3,2,1,0:T(2,128)S(1)}, u32[]{:S(2)}, u32[]{:S(2)}) async-start(f32[128,1,1,2,1024]{4,3,2,1,0:T(2,128)} %copy.31), calls=%async_computation.1 | async-start | bytes 2097152 | tf_op jit(solution)/shard_map/all_to_all | solution.py:27
  37.6 0.8 sub.60
  39.0 17.6 %all-to-all-done.1 = f32[128,1,1,2,1024]{4,3,2,1,0:T(2,128)S(1)} async-done(((f32[128,1,1,2,1024]{4,3,2,1,0:T(2,128)}), f32[128,1,1,2,1024]{4,3,2,1,0:T(2,128)S(1)}, u32[]{:S(2)}, u32[]{:S(2)}) %all-to-all-start.1) | async-done | bytes 1048608 | tf_op jit(solution)/shard_map/all_to_all | solution.py:27
  56.6 4.6 %all-to-all-start.2 = ((s32[128,1,1,2]{3,2,1,0:T(1,128)}), s32[128,1,1,2]{3,2,1,0:T(1,128)S(1)}, u32[]{:S(2)}, u32[]{:S(2)}) async-start(s32[128,1,1,2]{3,2,1,0:T(1,128)} %bitcast.31), calls=%async_computation.2 | async-start | bytes 131072 | tf_op jit(solution)/shard_map/all_to_all | solution.py:27
  61.2 0.7 reshape_reshape.12
  62.6 1.3 bitcast_dynamic-update-slice_fusion.2
  64.1 3.4 %fusion.4 = f32[128,8,128]{2,1,0:T(8,128)S(1)} fusion(bf16[4,128,128,128]{3,2,1,0:T(8,128)(2,1)} %param.9, bf16[128,8,128]{2,0,1:T(8,128)(2,1)S(1)} %convolution_convert_fusion.2), kind=kOutput, calls=%fused_computation.4 | convolution fusion | flops 33554432 | bytes 4980736 | tf_op jit(solution)/shard_map/krb,kbc->krc/dot_general | solution.py:66
  67.6 0.6 convolution_bitcast_fusion.2
  68.2 1.8 copy.35
  70.0 0.7 all-to-all-done.2
  70.7 9.2 %all-to-all-start.3 = ((f32[128,1,1,2,1024]{4,3,2,1,0:T(2,128)}), f32[128,1,1,2,1024]{4,3,2,1,0:T(2,128)S(1)}, u32[]{:S(2)}, u32[]{:S(2)}) async-start(f32[128,1,1,2,1024]{4,3,2,1,0:T(2,128)} %copy.35), calls=%async_computation.3 | async-start | bytes 2097152 | tf_op jit(solution)/shard_map/all_to_all | solution.py:27
  80.1 0.8 sub.65
  80.9 0.7 iota_compare_fusion.22
  81.7 17.5 %all-to-all-done.3 = f32[128,1,1,2,1024]{4,3,2,1,0:T(2,128)S(1)} async-done(((f32[128,1,1,2,1024]{4,3,2,1,0:T(2,128)}), f32[128,1,1,2,1024]{4,3,2,1,0:T(2,128)S(1)}, u32[]{:S(2)}, u32[]{:S(2)}) %all-to-all-start.3) | async-done | bytes 1048608 | tf_op jit(solution)/shard_map/all_to_all | solution.py:27
  99.1 4.6 %all-to-all-start.4 = ((s32[128,1,1,2]{3,2,1,0:T(1,128)}), s32[128,1,1,2]{3,2,1,0:T(1,128)S(1)}, u32[]{:S(2)}, u32[]{:S(2)}) async-start(s32[128,1,1,2]{3,2,1,0:T(1,128)} %bitcast.52), calls=%async_computation.4 | async-start | bytes 131072 | tf_op jit(solution)/shard_map/all_to_all | solution.py:27
  103.8 0.7 reshape_reshape.13
  105.1 1.3 bitcast_dynamic-update-slice_fusion.1
  106.7 3.4 %fusion.2 = f32[128,8,128]{2,1,0:T(8,128)S(1)} fusion(bf16[4,128,128,128]{3,2,1,0:T(8,128)(2,1)} %param.9, bf16[128,8,128]{2,0,1:T(8,128)(2,1)S(1)} %convolution_convert_fusion.1), kind=kOutput, calls=%fused_computation.2 | convolution fusion | flops 33554432 | bytes 4980736 | tf_op jit(solution)/shard_map/krb,kbc->krc/dot_general | solution.py:66
  110.1 0.6 convolution_bitcast_fusion.1
  110.8 1.8 copy.39
  112.6 0.7 all-to-all-done.4
  113.2 9.2 %all-to-all-start.5 = ((f32[128,1,1,2,1024]{4,3,2,1,0:T(2,128)}), f32[128,1,1,2,1024]{4,3,2,1,0:T(2,128)S(1)}, u32[]{:S(2)}, u32[]{:S(2)}) async-start(f32[128,1,1,2,1024]{4,3,2,1,0:T(2,128)} %copy.39), calls=%async_computation.5 | async-start | bytes 2097152 | tf_op jit(solution)/shard_map/all_to_all | solution.py:27
  122.6 0.8 sub.70
  123.4 0.7 iota_compare_fusion.21
  124.2 17.5 %all-to-all-done.5 = f32[128,1,1,2,1024]{4,3,2,1,0:T(2,128)S(1)} async-done(((f32[128,1,1,2,1024]{4,3,2,1,0:T(2,128)}), f32[128,1,1,2,1024]{4,3,2,1,0:T(2,128)S(1)}, u32[]{:S(2)}, u32[]{:S(2)}) %all-to-all-start.5) | async-done | bytes 1048608 | tf_op jit(solution)/shard_map/all_to_all | solution.py:27
  141.7 4.6 %all-to-all-start.6 = ((s32[128,1,1,2]{3,2,1,0:T(1,128)}), s32[128,1,1,2]{3,2,1,0:T(1,128)S(1)}, u32[]{:S(2)}, u32[]{:S(2)}) async-start(s32[128,1,1,2]{3,2,1,0:T(1,128)} %bitcast.73), calls=%async_computation.6 | async-start | bytes 131072 | tf_op jit(solution)/shard_map/all_to_all | solution.py:27
  146.3 0.7 reshape_reshape.14
  147.6 1.3 bitcast_dynamic-update-slice_fusion
  149.2 3.4 %fusion = f32[128,8,128]{2,1,0:T(8,128)S(1)} fusion(bf16[4,128,128,128]{3,2,1,0:T(8,128)(2,1)} %param.9, bf16[128,8,128]{2,0,1:T(8,128)(2,1)S(1)} %convolution_convert_fusion), kind=kOutput, calls=%fused_computation | convolution fusion | flops 33554432 | bytes 4980736 | tf_op jit(solution)/shard_map/krb,kbc->krc/dot_general | solution.py:66
  152.7 0.6 convolution_bitcast_fusion
  153.3 1.8 copy.43
  155.1 0.7 all-to-all-done.6
  155.8 9.2 %all-to-all-start.7 = ((f32[128,1,1,2,1024]{4,3,2,1,0:T(2,128)}), f32[128,1,1,2,1024]{4,3,2,1,0:T(2,128)S(1)}, u32[]{:S(2)}, u32[]{:S(2)}) async-start(f32[128,1,1,2,1024]{4,3,2,1,0:T(2,128)} %copy.43), calls=%async_computation.7 | async-start | bytes 2097152 | tf_op jit(solution)/shard_map/all_to_all | solution.py:27
  165.7 18.5 %all-to-all-done.7 = f32[128,1,1,2,1024]{4,3,2,1,0:T(2,128)S(1)} async-done(((f32[128,1,1,2,1024]{4,3,2,1,0:T(2,128)}), f32[128,1,1,2,1024]{4,3,2,1,0:T(2,128)S(1)}, u32[]{:S(2)}, u32[]{:S(2)}) %all-to-all-start.7) | async-done | bytes 1048608 | tf_op jit(solution)/shard_map/all_to_all | solution.py:27
  184.2 0.7 reshape_reshape.15
  185.5 1.9 %fusion.13 = f32[5,16,8,128]{3,2,1,0:T(8,128)} fusion(f32[5,16,8,128]{3,2,1,0:T(8,128)} %copy-done.1, bf16[16,8,128]{2,1,0:T(8,128)(2,1)S(1)} %fusion.34, bf16[5,16,128,128]{3,2,1,0:T(8,128)(2,1)} %param.8, pred[16]{0:T(512)(128)(4,1)S(1)} %iota_compare_fusion.20), kind=kOutput, calls=%fused_computation.24 | convolution fusion | flops 4210688 | bytes 622608 | tf_op jit(solution)/shard_map/srb,sbc->src/dot_general | solution.py:53
  (56 shorter events, 8.1 us)
Async XLA Ops:
  5.7 22.0 %all-to-all-start = ((s32[128,1,1,2]{3,2,1,0:T(1,128)}), s32[128,1,1,2]{3,2,1,0:T(1,128)S(1)}, u32[]{:S(2)}, u32[]{:S(2)}) async-start(s32[128,1,1,2]{3,2,1,0:T(1,128)} %bitcast.10), calls=%async_computation | async-start | bytes 131072 | tf_op jit(solution)/shard_map/all_to_all | solution.py:27
  25.9 36.7 %copy-start = (f32[5,16,8,128]{3,2,1,0:T(8,128)S(1)}, f32[5,16,8,128]{3,2,1,0:T(8,128)}, u32[]{:S(2)}) copy-start(f32[5,16,8,128]{3,2,1,0:T(8,128)} %param.7) | copy-start | bytes 983044
  27.7 29.0 %all-to-all-start.1 = ((f32[128,1,1,2,1024]{4,3,2,1,0:T(2,128)}), f32[128,1,1,2,1024]{4,3,2,1,0:T(2,128)S(1)}, u32[]{:S(2)}, u32[]{:S(2)}) async-start(f32[128,1,1,2,1024]{4,3,2,1,0:T(2,128)} %copy.31), calls=%async_computation.1 | async-start | bytes 2097152 | tf_op jit(solution)/shard_map/all_to_all | solution.py:27
  56.6 14.1 %all-to-all-start.2 = ((s32[128,1,1,2]{3,2,1,0:T(1,128)}), s32[128,1,1,2]{3,2,1,0:T(1,128)S(1)}, u32[]{:S(2)}, u32[]{:S(2)}) async-start(s32[128,1,1,2]{3,2,1,0:T(1,128)} %bitcast.31), calls=%async_computation.2 | async-start | bytes 131072 | tf_op jit(solution)/shard_map/all_to_all | solution.py:27
  70.7 28.4 %all-to-all-start.3 = ((f32[128,1,1,2,1024]{4,3,2,1,0:T(2,128)}), f32[128,1,1,2,1024]{4,3,2,1,0:T(2,128)S(1)}, u32[]{:S(2)}, u32[]{:S(2)}) async-start(f32[128,1,1,2,1024]{4,3,2,1,0:T(2,128)} %copy.35), calls=%async_computation.3 | async-start | bytes 2097152 | tf_op jit(solution)/shard_map/all_to_all | solution.py:27
  99.1 14.1 %all-to-all-start.4 = ((s32[128,1,1,2]{3,2,1,0:T(1,128)}), s32[128,1,1,2]{3,2,1,0:T(1,128)S(1)}, u32[]{:S(2)}, u32[]{:S(2)}) async-start(s32[128,1,1,2]{3,2,1,0:T(1,128)} %bitcast.52), calls=%async_computation.4 | async-start | bytes 131072 | tf_op jit(solution)/shard_map/all_to_all | solution.py:27
  113.2 28.4 %all-to-all-start.5 = ((f32[128,1,1,2,1024]{4,3,2,1,0:T(2,128)}), f32[128,1,1,2,1024]{4,3,2,1,0:T(2,128)S(1)}, u32[]{:S(2)}, u32[]{:S(2)}) async-start(f32[128,1,1,2,1024]{4,3,2,1,0:T(2,128)} %copy.39), calls=%async_computation.5 | async-start | bytes 2097152 | tf_op jit(solution)/shard_map/all_to_all | solution.py:27
  141.7 14.2 %all-to-all-start.6 = ((s32[128,1,1,2]{3,2,1,0:T(1,128)}), s32[128,1,1,2]{3,2,1,0:T(1,128)S(1)}, u32[]{:S(2)}, u32[]{:S(2)}) async-start(s32[128,1,1,2]{3,2,1,0:T(1,128)} %bitcast.73), calls=%async_computation.6 | async-start | bytes 131072 | tf_op jit(solution)/shard_map/all_to_all | solution.py:27
  148.9 6.2 %copy-start.1 = (f32[5,16,8,128]{3,2,1,0:T(8,128)}, f32[5,16,8,128]{3,2,1,0:T(8,128)S(1)}, u32[]{:S(2)}) copy-start(f32[5,16,8,128]{3,2,1,0:T(8,128)S(1)} %get-tuple-element.31) | copy-start | bytes 983044
  155.8 28.4 %all-to-all-start.7 = ((f32[128,1,1,2,1024]{4,3,2,1,0:T(2,128)}), f32[128,1,1,2,1024]{4,3,2,1,0:T(2,128)S(1)}, u32[]{:S(2)}, u32[]{:S(2)}) async-start(f32[128,1,1,2,1024]{4,3,2,1,0:T(2,128)} %copy.43), calls=%async_computation.7 | async-start | bytes 2097152 | tf_op jit(solution)/shard_map/all_to_all | solution.py:27
where the time goes:
time: 188 us; the launch traced here: 187 us
  waiting for transfers between devices  73 us (39%)
  starting transfers between devices  62.8 us (33%)
  matrix products  26.3 us (14%)
  local copies, waits for them, and re-layouts  17.2 us (9%)
  other arithmetic  7.72 us (4%)
    all_to_all x8, waiting for transfers between devices, one_exchange(): lax.all_to_all(pieces, axis, split_axis=0, concat_axis=0, tiled=True)  73 us
    all_to_all x8, starting transfers between devices, one_exchange(): lax.all_to_all(pieces, axis, split_axis=0, concat_axis=0, tiled=True)  62.8 us
    dot_general x4, matrix products, shards(): jnp.einsum('krb,kbc->krc', picked, off_blocks[level_at], preferred_elemen...  13.5 us
    dot_general x4, local copies, waits for them, and re-layouts, shards(): jnp.dot(packer.astype(jnp.float32), contribution, precision=lax.Precision...  7.2 us
    dot_general x5, matrix products, shards(): jnp.einsum('srb,sbc->src', work_rows, diag_inverse[level_at], preferred_e...  7.11 us
  transfers between devices with their start and end apart: 8, of which 7 were waited for; matrix products, arithmetic and copies ran while one was open for 23% of the time, Pallas kernels for 0%

commit v1 on v0

v1 whole, which is shorter than its diff:
```python
import functools

import jax
import jax.numpy as jnp
from jax import lax
from jax.experimental import pallas as pl
from jax.experimental.pallas import tpu as pltpu
from jax.sharding import PartitionSpec as P

CAP = 2
CHAINS = 4
CHUNKS = 8
AXES = ("gx", "gy", "gz")


def level_kernel(level, levels, slots, records, packed, *refs):
    first, last = level == 0, level == levels - 1
    refs = list(refs)
    counts = refs.pop(0)
    if not last:
        source, slot_of = refs.pop(0), refs.pop(0)
    if not first:
        labels, arrived = refs.pop(0), refs.pop(0)
        if level > 1:
            acc_in = refs.pop(0)
    rhs_hbm, diag_hbm = refs.pop(0), refs.pop(0)
    if not last:
        off_hbm = refs.pop(0)
    solved = refs.pop(0)
    if not last:
        outgoing = refs.pop(0)
        if not first:
            acc = refs.pop(0)
    elif not first:
        acc = refs.pop()
    rhs, diag, sems = refs.pop(0), refs.pop(0), refs.pop(0)
    rhs_copy = pltpu.make_async_copy(rhs_hbm.at[level], rhs, sems.at[0])
    diag_copy = pltpu.make_async_copy(diag_hbm.at[level], diag, sems.at[1])
    rhs_copy.start()
    diag_copy.start()
    off_copies = []
    if not last:
        off = refs.pop(0)
        span = records // CHUNKS
        for chunk in range(CHUNKS):
            rows = pl.ds(chunk * span, span)
            copy = pltpu.make_async_copy(off_hbm.at[level, rows], off.at[rows], sems.at[2 + chunk])
            copy.start()
            off_copies.append(copy)
    blocks = levels * slots + 1
    if not first:
        if level == 1:
            for chain in range(CHAINS):
                for block in range(level * slots, blocks):
                    acc[chain * blocks + block] = jnp.zeros(acc.shape[1:], jnp.float32)
        else:
            for chain in range(CHAINS):
                for block in range(level * slots, blocks):
                    acc[chain * blocks + block] = acc_in[chain * blocks + block]

        def add(step, carry):
            for chain in range(CHAINS):
                at = step * CHAINS + chain
                row = labels[level - 1, at] + chain * blocks
                acc[row] = acc[row] + arrived[at]
            return carry

        lax.fori_loop(0, packed // CHAINS, add, 0, unroll=16)
    rhs_copy.wait()
    diag_copy.wait()
    for slot in range(slots):
        work = rhs[slot]
        if not first:
            pending = acc[level * slots + slot]
            for chain in range(1, CHAINS):
                pending = pending + acc[chain * blocks + level * slots + slot]
            work = work - pending
        value = jnp.dot(work.astype(jnp.bfloat16), diag[slot], preferred_element_type=jnp.float32)
        solved[slot] = jnp.where(slot < counts[level, 0], value, jnp.float32(0.0))
    if not last:
        for record in range(records):
            if record % span == 0:
                off_copies[record // span].wait()
            picked = solved[source[level, record]].astype(jnp.bfloat16)
            outgoing[slot_of[level, record]] = jnp.dot(
                picked, off[record], preferred_element_type=jnp.float32
            )


def one_level(level, levels, slots, rhs_count, width, records, packed, args):
    first, last = level == 0, level == levels - 1
    smem = pl.BlockSpec(memory_space=pltpu.SMEM)
    vmem = pl.BlockSpec(memory_space=pltpu.VMEM)
    anywhere = pl.BlockSpec(memory_space=pltpu.HBM)
    in_specs = [smem]
    if not last:
        in_specs += [smem, smem]
    aliases = {}
    if not first:
        in_specs += [smem, vmem]
        if level > 1:
            in_specs += [vmem]
    in_specs += [anywhere, anywhere]
    if not last:
        in_specs += [anywhere]
    acc_shape = (CHAINS * (levels * slots + 1), rhs_count, width)
    shapes = [jax.ShapeDtypeStruct((slots, rhs_count, width), jnp.float32)]
    scratch = [
        pltpu.VMEM((slots, rhs_count, width), jnp.float32),
        pltpu.VMEM((slots, width, width), jnp.bfloat16),
        pltpu.SemaphoreType.DMA((2 + CHUNKS,)),
    ]
    if not last:
        shapes += [jax.ShapeDtypeStruct((packed, rhs_count, width), jnp.float32)]
        if not first:
            shapes += [jax.ShapeDtypeStruct(acc_shape, jnp.float32)]
        scratch += [pltpu.VMEM((records, width, width), jnp.bfloat16)]
    else:
        scratch += [pltpu.VMEM(acc_shape, jnp.float32)]
    return pl.pallas_call(
        functools.partial(level_kernel, level, levels, slots, records, packed),
        out_shape=shapes,
        in_specs=in_specs,
        out_specs=[vmem] * len(shapes),
        scratch_shapes=scratch,
        input_output_aliases=aliases,
        compiler_params=pltpu.CompilerParams(vmem_limit_bytes=48 * 1024 * 1024),
        name=f"level_{level}",
    )(*args)


def shards(
    right_side, diag_inverse, off_blocks, live_counts, source_slot, target_owner, target_block
):
    levels, slots, rhs_count, width = right_side.shape
    records = off_blocks.shape[1]
    owners = lax.axis_size(AXES)
    packed = owners * CAP
    order = jnp.arange(records, dtype=jnp.int32)
    same = (target_owner[:, :, None] == target_owner[:, None, :]) & (order[:, None] > order[None, :])
    position = jnp.sum(same.astype(jnp.int32), axis=2)
    slot_of = target_owner * CAP + position
    buffer_ids = jnp.arange(packed, dtype=jnp.int32)
    dummy = levels * slots
    hits = (buffer_ids[None, :, None] == slot_of[:, None, :]).astype(jnp.int32)
    labels = jnp.sum(hits * (target_block - dummy)[:, None, :], axis=2) + dummy
    labels = jnp.swapaxes(labels.reshape(levels - 1, owners, CAP), 0, 1)
    labels = lax.all_to_all(labels, AXES, 0, 0, tiled=True)
    labels = jnp.swapaxes(labels, 0, 1).reshape(levels - 1, packed)
    results = []
    arrived = acc = None
    for level in range(levels):
        last = level == levels - 1
        args = [live_counts]
        if not last:
            args += [source_slot, slot_of]
        if level > 0:
            args += [labels, arrived]
            if level > 1:
                args += [acc]
        args += [right_side, diag_inverse]
        if not last:
            args += [off_blocks]
        out = one_level(level, levels, slots, rhs_count, width, records, packed, args)
        results.append(out[0])
        if not last:
            outgoing = out[1].reshape(owners, CAP * rhs_count, width)
            arrived = lax.all_to_all(outgoing, AXES, 0, 0, tiled=True)
            arrived = arrived.reshape(packed, rhs_count, width)
            if level > 0:
                acc = out[2]
    return jnp.stack(results)


def solution(mesh):
    split = P(None, AXES, None, None)
    flat = P(None, AXES)
    return jax.shard_map(
        shards,
        mesh=mesh,
        in_specs=(split, split, split, flat, flat, flat, flat),
        out_specs=split,
        check_vma=False,
    )
```

time: 188 us -> 145 us (0.77)
  blocking collectives: 0 us -> 47.1 us
  starting transfers between devices: 62.8 us -> 26.5 us
  waiting for transfers between devices: 73 us -> 38.7 us
  matrix products: 26.3 us -> 0 us
  Pallas kernels: 0 us -> 21.2 us
  local copies, waits for them, and re-layouts: 17.2 us -> 9.08 us
  other arithmetic: 7.72 us -> 1.98 us
    all_to_all x0 -> x2, blocking collectives: none -> 47.1 us  [shards(): arrived = lax.all_to_all(outgoing, AXES, 0, 0, tiled=True)]
    all_to_all x8 -> x3, starting transfers between devices: 62.8 us -> 26.5 us  [the longest x2 15 us: shards(): arrived = lax.all_to_all(outgoing, AXES, 0, 0, tiled=True)]
    all_to_all x8 -> x3, waiting for transfers between devices: 73 us -> 38.7 us  [the longest x2 38 us: shards(): arrived = lax.all_to_all(outgoing, AXES, 0, 0, tiled=True)]
    dot_general x21 -> x0, matrix products: 26.3 us -> none  [the longest x4 13.5 us: shards(): jnp.einsum('krb,kbc->krc', picked, off_blocks[level_at], preferred_elemen...]
    pallas_call x0 -> x5, Pallas kernels: none -> 21.2 us  [one_level(): pl.pallas_call(functools.partial(level_kernel, level, levels, slots, reco...]
    unnamed x11 -> x25, local copies, waits for them, and re-layouts: 0.08 us -> 7.56 us
    dot_general x4 -> x0, local copies, waits for them, and re-layouts: 7.2 us -> none  [shards(): jnp.dot(packer.astype(jnp.float32), contribution, precision=lax.Precision...]
    lt x5 -> x0, other arithmetic: 3.15 us -> none  [shards(): slot_ids < live_counts[level_at, 0]]
  transfers between devices with their start and end apart: 8 -> 3, of which waited for: 7 -> 3; matrix products, arithmetic and copies ran while one was open for 23% -> 1% of each run, Pallas kernels for 0% -> 3%
where the time goes in v1:
time: 145 us
  blocking collectives  47.1 us (32%)
  waiting for transfers between devices  38.7 us (27%)
  starting transfers between devices  26.5 us (18%)
  Pallas kernels  21.2 us (15%)
  local copies, waits for them, and re-layouts  9.08 us (6%)
  other arithmetic  1.98 us (1%)
    all_to_all x2, blocking collectives, shards(): arrived = lax.all_to_all(outgoing, AXES, 0, 0, tiled=True)  47.1 us
    all_to_all x2, waiting for transfers between devices, shards(): arrived = lax.all_to_all(outgoing, AXES, 0, 0, tiled=True)  38 us
    pallas_call x5, Pallas kernels, one_level(): pl.pallas_call(functools.partial(level_kernel, level, levels, slots, reco...  21.2 us
    all_to_all x2, starting transfers between devices, shards(): arrived = lax.all_to_all(outgoing, AXES, 0, 0, tiled=True)  15 us
    all_to_all x1, starting transfers between devices, shards(): labels = lax.all_to_all(labels, AXES, 0, 0, tiled=True)  11.5 us
    unnamed x25, local copies, waits for them, and re-layouts  7.56 us
  transfers between devices with their start and end apart: 3, of which 3 were waited for; matrix products, arithmetic and copies ran while one was open for 1% of the time, Pallas kernels for 3%

profile of v1, /device:TPU:1, one launch (start us, length us, event | category | flops | bytes accessed | tf_op | source)
XLA Modules:
  0.0 144.7 jit_solution(3897722084979544180)
XLA Ops:
  0.0 1.0 convert_reduce_fusion
  1.0 0.7 multiply_add_fusion
  1.7 0.3 select_reduce_fusion
  2.0 0.8 copy.23
  2.8 11.5 %all-to-all-start = ((s32[128,4,2]{1,2,0:T(2,128)}), s32[128,4,2]{1,2,0:T(2,128)S(1)}, u32[]{:S(2)}, u32[]{:S(2)}) async-start(s32[128,4,2]{1,2,0:T(2,128)} %bitcast.2), calls=%async_computation | async-start | bytes 262144 | tf_op jit(solution)/shard_map/all_to_all | solution.py:148
  14.3 0.7 copy.22.refs_0_
  15.0 0.0 copy-start
  15.0 1.7 %copy-done = bf16[5,16,128,128]{3,2,1,0:T(8,128)(2,1)S(1)} copy-done((bf16[5,16,128,128]{3,2,1,0:T(8,128)(2,1)S(1)}, bf16[5,16,128,128]{3,2,1,0:T(8,128)(2,1)}, u32[]{:S(2)}) %copy-start) | copy-done | bytes 2621464
  16.8 0.0 copy-start.2
  16.8 1.0 copy-done.2
  17.7 0.0 copy-start.7
  17.8 0.7 copy-done.7
  18.4 4.9 %level_0.1 = (f32[16,8,128]{2,1,0:T(8,128)S(1)}, f32[256,8,128]{2,1,0:T(8,128)}) custom-call(s32[5,1]{1,0:T(8,128)S(1)} %copy.22.refs_0_, s32[4,128]{1,0:T(4,128)S(1)} %copy-done.7, s32[4,128]{1,0:T(4,128)S(1)} %get-tuple-element.27.refs_2_, f32[5,16,8,128]{3,2,1,0:T(8,128)S(1)} %copy-done.2, bf16[5,16,128,128]{3,2,1,0:T(8,128)(2,1)S(1)} %copy-done, ...), custom_call_target="tpu_custom_call" | custom-call | tf_op jit(solution)/shard_map/level_0/pallas_call | solution.py:120
  23.4 0.0 copy-start.3
  23.4 0.0 copy-start.8
  23.4 0.7 all-to-all-done
  24.0 9.1 %all-to-all-start.1 = ((f32[128,16,128]{2,1,0:T(8,128)}), f32[128,16,128]{2,1,0:T(8,128)S(1)}, u32[]{:S(2)}, u32[]{:S(2)}) async-start(f32[128,16,128]{2,1,0:T(8,128)} %bitcast.5), calls=%async_computation.1 | async-start | bytes 2097152 | tf_op jit(solution)/shard_map/all_to_all | solution.py:168
  33.2 0.1 copy.25.refs_3_.refs_1_
  33.2 19.1 %all-to-all-done.1 = f32[128,16,128]{2,1,0:T(8,128)S(1)} async-done(((f32[128,16,128]{2,1,0:T(8,128)}), f32[128,16,128]{2,1,0:T(8,128)S(1)}, u32[]{:S(2)}, u32[]{:S(2)}) %all-to-all-start.1) | async-done | bytes 1048608 | tf_op jit(solution)/shard_map/all_to_all | solution.py:168
  52.4 0.0 copy-done.3
  52.4 0.0 copy-done.8
  52.4 4.5 %level_1.1 = (f32[16,8,128]{2,1,0:T(8,128)S(1)}, f32[256,8,128]{2,1,0:T(8,128)S(1)}, f32[324,8,128]{2,1,0:T(8,128)S(1)}) custom-call(s32[5,1]{1,0:T(8,128)S(1)} %copy.22.refs_0_, s32[4,128]{1,0:T(4,128)S(1)} %copy-done.8, s32[4,128]{1,0:T(4,128)S(1)} %get-tuple-element.27.refs_2_, s32[4,256]{1,0:T(4,128)S(1)} %copy.25.refs_3_.refs_1_, ...), custom_call_target="tpu_custom_call" | custom-call | tf_op jit(solution)/shard_map/level_1/pallas_call | solution.py:120
  56.9 23.5 %all_to_all.25 = f32[128,16,128]{2,1,0:T(8,128)S(1)} all-to-all(f32[128,16,128]{2,1,0:T(8,128)S(1)} %bitcast.29), channel_id=1, replica_groups=mesh['gx'=4,'gy'=4,'gz'=8] {'gx','gy','gz'}, dimensions={0} | all-to-all | bytes 2097152 | tf_op jit(solution)/shard_map/all_to_all | solution.py:168
  80.4 4.5 %level_2.1 = (f32[16,8,128]{2,1,0:T(8,128)S(1)}, f32[256,8,128]{2,1,0:T(8,128)S(1)}, f32[324,8,128]{2,1,0:T(8,128)S(1)}) custom-call(s32[5,1]{1,0:T(8,128)S(1)} %copy.22.refs_0_, s32[4,128]{1,0:T(4,128)S(1)} %copy-done.8, s32[4,128]{1,0:T(4,128)S(1)} %get-tuple-element.27.refs_2_, s32[4,256]{1,0:T(4,128)S(1)} %copy.25.refs_3_.refs_1_, ...), custom_call_target="tpu_custom_call" | custom-call | tf_op jit(solution)/shard_map/level_2/pallas_call | solution.py:120
  85.0 23.6 %all_to_all.26 = f32[128,16,128]{2,1,0:T(8,128)S(1)} all-to-all(f32[128,16,128]{2,1,0:T(8,128)S(1)} %bitcast.28), channel_id=1, replica_groups=mesh['gx'=4,'gy'=4,'gz'=8] {'gx','gy','gz'}, dimensions={0} | all-to-all | bytes 2097152 | tf_op jit(solution)/shard_map/all_to_all | solution.py:168
  108.5 4.5 %level_3.1 = (f32[16,8,128]{2,1,0:T(8,128)S(1)}, f32[256,8,128]{2,1,0:T(8,128)S(1)}, f32[324,8,128]{2,1,0:T(8,128)S(1)}) custom-call(s32[5,1]{1,0:T(8,128)S(1)} %copy.22.refs_0_, s32[4,128]{1,0:T(4,128)S(1)} %copy-done.8, s32[4,128]{1,0:T(4,128)S(1)} %get-tuple-element.27.refs_2_, s32[4,256]{1,0:T(4,128)S(1)} %copy.25.refs_3_.refs_1_, ...), custom_call_target="tpu_custom_call" | custom-call | tf_op jit(solution)/shard_map/level_3/pallas_call | solution.py:120
  113.1 0.0 copy-start.4
  113.1 1.1 copy-done.4
  114.1 0.0 copy-start.6
  114.1 1.0 copy-done.6
  115.1 0.0 copy-start.1
  115.1 5.9 %all-to-all-start.4 = ((f32[128,16,128]{2,1,0:T(8,128)}), f32[128,16,128]{2,1,0:T(8,128)}, u32[]{:S(2)}, u32[]{:S(2)}) async-start(f32[128,16,128]{2,1,0:T(8,128)} %bitcast.27), calls=%async_computation.4 | async-start | bytes 2097152 | tf_op jit(solution)/shard_map/all_to_all | solution.py:168
  121.1 0.0 copy-start.9
  121.1 18.9 %all-to-all-done.4 = f32[128,16,128]{2,1,0:T(8,128)} async-done(((f32[128,16,128]{2,1,0:T(8,128)}), f32[128,16,128]{2,1,0:T(8,128)}, u32[]{:S(2)}, u32[]{:S(2)}) %all-to-all-start.4) | async-done | bytes 1048608 | tf_op jit(solution)/shard_map/all_to_all | solution.py:168
  140.0 0.0 copy-done.1
  140.0 0.0 copy-start.5
  140.0 1.3 copy-done.5
  141.3 2.7 %level_4.1 = f32[16,8,128]{2,1,0:T(8,128)S(1)} custom-call(s32[5,1]{1,0:T(8,128)S(1)} %copy.22.refs_0_, s32[4,256]{1,0:T(4,128)S(1)} %copy.25.refs_3_.refs_1_, f32[256,8,128]{2,1,0:T(8,128)} %bitcast.15.refs_2_, f32[324,8,128]{2,1,0:T(8,128)S(1)} %copy-done.5, f32[5,16,8,128]{3,2,1,0:T(8,128)S(1)} %copy-done.3, bf16[5,16,128,128]{3,2,1,0:T(8,128)(2,1)S(1)} %copy-done.1), custom_call_target="tpu_custom_call" | custom-call | tf_op jit(solution)/shard_map/level_4/pallas_call | solution.py:120
  144.0 0.0 copy-done.9
  144.0 0.6 bitcast_dynamic-update-slice_fusion
  (6 shorter events, 0.0 us)
Async XLA Ops:
  2.8 21.2 %all-to-all-start = ((s32[128,4,2]{1,2,0:T(2,128)}), s32[128,4,2]{1,2,0:T(2,128)S(1)}, u32[]{:S(2)}, u32[]{:S(2)}) async-start(s32[128,4,2]{1,2,0:T(2,128)} %bitcast.2), calls=%async_computation | async-start | bytes 262144 | tf_op jit(solution)/shard_map/all_to_all | solution.py:148
  15.0 1.7 %copy-start = (bf16[5,16,128,128]{3,2,1,0:T(8,128)(2,1)S(1)}, bf16[5,16,128,128]{3,2,1,0:T(8,128)(2,1)}, u32[]{:S(2)}) copy-start(bf16[5,16,128,128]{3,2,1,0:T(8,128)(2,1)} %refs_5_.5) | copy-start | bytes 7864324
  16.8 1.0 copy-start.2
  17.7 0.7 copy-start.7
  23.4 29.0 %copy-start.3 = (f32[5,16,8,128]{3,2,1,0:T(8,128)S(1)}, f32[5,16,8,128]{3,2,1,0:T(8,128)}, u32[]{:S(2)}) copy-start(f32[5,16,8,128]{3,2,1,0:T(8,128)} %refs_4_.3) | copy-start | bytes 983044
  23.4 29.0 %copy-start.8 = (s32[4,128]{1,0:T(4,128)S(1)}, s32[4,128]{1,0:T(4,128)}, u32[]{:S(2)}) copy-start(s32[4,128]{1,0:T(4,128)} %refs_1_.7) | copy-start | bytes 6148
  24.0 28.3 %all-to-all-start.1 = ((f32[128,16,128]{2,1,0:T(8,128)}), f32[128,16,128]{2,1,0:T(8,128)S(1)}, u32[]{:S(2)}, u32[]{:S(2)}) async-start(f32[128,16,128]{2,1,0:T(8,128)} %bitcast.5), calls=%async_computation.1 | async-start | bytes 2097152 | tf_op jit(solution)/shard_map/all_to_all | solution.py:168
  113.1 1.1 copy-start.4
  114.1 1.0 copy-start.6
  115.1 24.9 %copy-start.1 = (bf16[5,16,128,128]{3,2,1,0:T(8,128)(2,1)S(1)}, bf16[5,16,128,128]{3,2,1,0:T(8,128)(2,1)}, u32[]{:S(2)}) copy-start(bf16[5,16,128,128]{3,2,1,0:T(8,128)(2,1)} %refs_5_.5) | copy-start | bytes 7864324
  115.1 24.9 %all-to-all-start.4 = ((f32[128,16,128]{2,1,0:T(8,128)}), f32[128,16,128]{2,1,0:T(8,128)}, u32[]{:S(2)}, u32[]{:S(2)}) async-start(f32[128,16,128]{2,1,0:T(8,128)} %bitcast.27), calls=%async_computation.4 | async-start | bytes 2097152 | tf_op jit(solution)/shard_map/all_to_all | solution.py:168
  121.1 23.0 %copy-start.9 = (f32[5,16,8,128]{3,2,1,0:T(8,128)}, f32[5,16,8,128]{3,2,1,0:T(8,128)S(1)}, u32[]{:S(2)}) copy-start(f32[5,16,8,128]{3,2,1,0:T(8,128)S(1)} %bitcast_dynamic-update-slice_fusion.1) | copy-start | bytes 983044
  140.0 1.3 copy-start.5

commit v2 on v0

v2 whole, which is shorter than its diff:
```python
import functools

import jax
import jax.numpy as jnp
from jax import lax
from jax.experimental import pallas as pl
from jax.experimental.pallas import tpu as pltpu
from jax.sharding import PartitionSpec as P

CAP = 2
CHAINS = 4
CHUNKS = 8
AXES = ("gx", "gy", "gz")
VMEM = pl.BlockSpec(memory_space=pltpu.VMEM)
HBM = pl.BlockSpec(memory_space=pltpu.HBM)
CONTRACT_LANES = (((1,), (1,)), ((), ()))


def solve(level, rhs, diag, counts, accs, solved):
    slots = solved.shape[0]
    live = jnp.broadcast_to(counts[:, level : level + 1], solved.shape[1:])
    for slot in range(slots):
        work = rhs[slot]
        if accs:
            at = level * slots + slot
            work = work - ((accs[0][at] + accs[1][at]) + (accs[2][at] + accs[3][at]))
        value = jnp.dot(work.astype(jnp.bfloat16), diag[slot], preferred_element_type=jnp.float32)
        solved[slot] = jnp.where(live > slot, value, jnp.float32(0.0))


class Level:
    def __init__(self, level, rhs_hbm, diag_hbm, off_hbm, rhs, diag, off, sems):
        self.parts = [
            pltpu.make_async_copy(rhs_hbm.at[level], rhs, sems.at[0]),
            pltpu.make_async_copy(diag_hbm.at[level], diag, sems.at[1]),
        ]
        self.chunks = []
        if off is not None:
            self.span = off.shape[0] // CHUNKS
            for chunk in range(CHUNKS):
                rows = pl.ds(chunk * self.span, self.span)
                self.chunks.append(
                    pltpu.make_async_copy(off_hbm.at[level, rows], off.at[rows], sems.at[2 + chunk])
                )
        for copy in self.parts + self.chunks:
            copy.start()

    def wait_diagonal(self):
        for copy in self.parts:
            copy.wait()

    def wait_record(self, record):
        if record % self.span == 0:
            self.chunks[record // self.span].wait()


def contribute(loaded, off, solved, source_smem, level, store):
    for record in range(off.shape[0]):
        loaded.wait_record(record)
        picked = solved[source_smem[level, record]].astype(jnp.bfloat16)
        store(record, jnp.dot(picked, off[record], preferred_element_type=jnp.float32))


def first_kernel(
    dummy, counts_hbm, source_hbm, owner_hbm, block_hbm, rhs_hbm, diag_hbm, off_hbm,
    solved, outgoing, slot_table, counts, source, acc_0, acc_1, acc_2, acc_3,
    rhs, diag, off, owner, block, row_vmem, row_smem, source_smem, table_sems, sems,
):
    tables = ((owner_hbm, owner), (block_hbm, block), (counts_hbm, counts), (source_hbm, source))
    tables = [
        pltpu.make_async_copy(table, held, table_sems.at[2 + at])
        for at, (table, held) in enumerate(tables)
    ]
    for copy in tables:
        copy.start()
    source_copy = pltpu.make_async_copy(source_hbm, source_smem, table_sems.at[0])
    row_copy = pltpu.make_async_copy(row_vmem, row_smem, table_sems.at[1])
    source_copy.start()
    loaded = Level(0, rhs_hbm, diag_hbm, off_hbm, rhs, diag, off, sems)
    for acc in (acc_0, acc_1, acc_2, acc_3):
        for row in range(acc.shape[0]):
            acc[row] = jnp.zeros(acc.shape[1:], jnp.float32)
    for copy in tables:
        copy.wait()
    exchanges, width = owner.shape
    owners = width
    stride = outgoing.shape[0] // owners
    height = solved.shape[1]
    down = lax.broadcasted_iota(jnp.int32, (owners, width), 0)
    along = lax.broadcasted_iota(jnp.int32, (owners, width), 1)
    before = (down < along).astype(jnp.bfloat16)
    labels = jnp.full((owners, width), dummy, jnp.float32)
    for level in range(exchanges):
        owner_now = owner[level : level + 1, :]
        hit = (down == owner_now).astype(jnp.float32)
        hit_low = hit.astype(jnp.bfloat16)
        earlier = jnp.dot(hit_low, before, preferred_element_type=jnp.float32)
        position = jnp.sum(hit * earlier, axis=0, keepdims=True)
        place = position.astype(jnp.int32)
        slot_table[level : level + 1, :] = owner_now * CAP + place
        if level == 0:
            row_vmem[...] = owner_now * stride + place * height
            row_copy.start()
        value = (block[level : level + 1, :] - dummy).astype(jnp.float32)
        spread = jnp.where(
            down == CAP * level,
            value * (1.0 - position),
            jnp.where(down == CAP * level + 1, value * position, 0.0),
        ).astype(jnp.bfloat16)
        labels = labels + lax.dot_general(
            hit_low, spread, CONTRACT_LANES, preferred_element_type=jnp.float32
        )
    outgoing[pl.ds(CAP * height, owners, stride=stride), :] = labels
    loaded.wait_diagonal()
    solve(0, rhs, diag, counts, None, solved)
    source_copy.wait()
    row_copy.wait()

    def store(record, value):
        outgoing[pl.ds(row_smem[0, record], height), :] = value

    contribute(loaded, off, solved, source_smem, 0, store)


def later_kernel(level, levels, *refs):
    last = level == levels - 1
    refs = list(refs)
    take = lambda count: [refs.pop(0) for _ in range(count)]
    counts, arrived = take(2)
    accs = take(CHAINS)
    label_table = take(1)[0] if level > 1 else None
    rhs_hbm, diag_hbm = take(2)
    if not last:
        source, slot_table, off_hbm, solved, outgoing = take(5)
        accs = take(CHAINS)
        if level == 1:
            label_table = take(1)[0]
        off, source_smem, slot_smem = take(3)
    else:
        earlier = take(level)
        result, solved = take(2)
        off = off_hbm = None
    rhs, diag, label_smem, table_sems, sems = refs
    height, width = solved.shape[1:]
    owners = label_smem.shape[1]
    stride = arrived.shape[0] // owners
    copies = []
    if level == 1:
        rows = arrived[pl.ds(CAP * height, owners, stride=stride), :].astype(jnp.bfloat16)
        down = lax.broadcasted_iota(jnp.int32, (label_table.shape[0], width), 0)
        along = lax.broadcasted_iota(jnp.int32, (label_table.shape[0], width), 1)
        turned = lax.dot_general(
            (down == along).astype(jnp.bfloat16),
            rows,
            CONTRACT_LANES,
            preferred_element_type=jnp.float32,
        )
        label_table[...] = turned.astype(jnp.int32)
    label_copy = pltpu.make_async_copy(label_table, label_smem, table_sems.at[0])
    label_copy.start()
    loaded = Level(level, rhs_hbm, diag_hbm, off_hbm, rhs, diag, off, sems)
    if not last:
        for at, (table, scalars) in enumerate(((source, source_smem), (slot_table, slot_smem))):
            copies.append(pltpu.make_async_copy(table, scalars, table_sems.at[1 + at]))
    else:
        for at, piece in enumerate(earlier):
            copies.append(pltpu.make_async_copy(piece, result.at[at], table_sems.at[1 + at]))
    for copy in copies:
        copy.start()
    label_copy.wait()
    for sender in range(owners):
        for place in range(CAP):
            acc = accs[(sender % 2) * CAP + place]
            row = label_smem[CAP * (level - 1) + place, sender]
            at = sender * stride + place * height
            acc[row] = acc[row] + arrived[at : at + height, :]
    loaded.wait_diagonal()
    solve(level, rhs, diag, counts, accs, solved)
    if last:
        copy = pltpu.make_async_copy(solved, result.at[level], table_sems.at[1 + level])
        copy.start()
        copies.append(copy)
    for copy in copies:
        copy.wait()
    if not last:

        def store(record, value):
            outgoing[slot_smem[level, record]] = value

        contribute(loaded, off, solved, source_smem, level, store)


def shards(
    right_side, diag_inverse, off_blocks, live_counts, source_slot, target_owner, target_block
):
    levels, slots, height, width = right_side.shape
    exchanges, records = off_blocks.shape[:2]
    owners = lax.axis_size(AXES)
    dummy = levels * slots
    counts = live_counts.T
    stride = CAP * height + 1
    in_hbm = lambda x: pltpu.with_memory_space_constraint(x, pltpu.HBM)
    right_side, diag_inverse, off_blocks = map(in_hbm, (right_side, diag_inverse, off_blocks))
    tables = list(map(in_hbm, (counts, source_slot, target_owner, target_block)))
    table_shape = pltpu.VMEM((exchanges, records), jnp.int32)
    params = pltpu.CompilerParams(vmem_limit_bytes=24 * 1024 * 1024)
    acc_shapes = [pltpu.VMEM((dummy + 1, height, width), jnp.float32)] * CHAINS
    solved_shape = pltpu.VMEM((slots, height, width), jnp.float32)
    level_scratch = [
        pltpu.VMEM((slots, height, width), jnp.float32),
        pltpu.VMEM((slots, width, width), jnp.bfloat16),
    ]
    off_scratch = pltpu.VMEM((records, width, width), jnp.bfloat16)
    table_scratch = pltpu.SMEM((exchanges, records), jnp.int32)
    level_sems = pltpu.SemaphoreType.DMA((2 + CHUNKS,))
    out = pl.pallas_call(
        functools.partial(first_kernel, dummy),
        out_shape=[
            solved_shape,
            pltpu.VMEM((owners * stride, width), jnp.float32),
            table_shape,
            pltpu.VMEM(counts.shape, jnp.int32),
            table_shape,
            *acc_shapes,
        ],
        in_specs=[HBM] * 7,
        out_specs=[VMEM] * (5 + CHAINS),
        scratch_shapes=[
            *level_scratch,
            off_scratch,
            table_shape,
            table_shape,
            pltpu.VMEM((1, records), jnp.int32),
            pltpu.SMEM((1, records), jnp.int32),
            table_scratch,
            pltpu.SemaphoreType.DMA((6,)),
            level_sems,
        ],
        compiler_params=params,
        name="level_0",
    )(*tables, right_side, diag_inverse, off_blocks)
    solved, outgoing, slot_table, counts, source_slot = out[:5]
    accs = out[5:]
    outgoing = outgoing.reshape(owners, stride, 1, width)
    arrived = lax.all_to_all(outgoing, AXES, 0, 0, tiled=True).reshape(owners * stride, width)
    results = [solved]
    label_table = None
    label_shape = (CAP * exchanges, owners)
    for level in range(1, levels):
        last = level == levels - 1
        args = [counts, arrived, *accs]
        specs = [VMEM] * (2 + CHAINS)
        if level > 1:
            args += [label_table]
            specs += [VMEM]
        args += [right_side, diag_inverse]
        specs += [HBM] * 2
        tail = [*level_scratch, pltpu.SMEM(label_shape, jnp.int32)]
        aliases = {}
        if not last:
            args += [source_slot, slot_table, off_blocks]
            specs += [VMEM, VMEM, HBM]
            shapes = [
                solved_shape,
                pltpu.VMEM((owners * CAP, height, width), jnp.float32),
                *acc_shapes,
            ]
            aliases = {2 + chain: 2 + chain for chain in range(CHAINS)}
            if level == 1:
                shapes += [pltpu.VMEM(label_shape, jnp.int32)]
            out_specs = [VMEM] * len(shapes)
            scratch = [off_scratch, table_scratch, table_scratch] + tail
            scratch += [pltpu.SemaphoreType.DMA((3,)), level_sems]
        else:
            args += results
            specs += [VMEM] * level
            shapes = jax.ShapeDtypeStruct((levels, slots, height, width), jnp.float32)
            out_specs = HBM
            scratch = [pltpu.VMEM((slots, height, width), jnp.float32)] + tail
            scratch += [pltpu.SemaphoreType.DMA((2 + level,)), pltpu.SemaphoreType.DMA((2,))]
        out = pl.pallas_call(
            functools.partial(later_kernel, level, levels),
            out_shape=shapes,
            in_specs=specs,
            out_specs=out_specs,
            scratch_shapes=scratch,
            input_output_aliases=aliases,
            compiler_params=params,
            name=f"level_{level}",
        )(*args)
        if last:
            return out
        solved, outgoing = out[:2]
        accs = out[2 : 2 + CHAINS]
        if level == 1:
            label_table = out[2 + CHAINS]
        results.append(solved)
        outgoing = outgoing.reshape(owners, CAP * height, width)
        arrived = lax.all_to_all(outgoing, AXES, 0, 0, tiled=True)
        arrived = arrived.reshape(owners * CAP * height, width)


def solution(mesh):
    split = P(None, AXES, None, None)
    flat = P(None, AXES)
    return jax.shard_map(
        shards,
        mesh=mesh,
        in_specs=(split, split, split, flat, flat, flat, flat),
        out_specs=split,
        check_vma=False,
    )
```

time: 188 us -> 120 us (0.64)
  blocking collectives: 0 us -> 102 us
  waiting for transfers between devices: 73 us -> 0 us
  starting transfers between devices: 62.8 us -> 0 us
  matrix products: 26.3 us -> 0 us
  Pallas kernels: 0 us -> 17.6 us
  local copies, waits for them, and re-layouts: 17.2 us -> 0 us
  other arithmetic: 7.72 us -> 0 us
    all_to_all x0 -> x4, blocking collectives: none -> 102 us  [the longest x3 70.6 us: shards(): arrived = lax.all_to_all(outgoing, AXES, 0, 0, tiled=True)]
    all_to_all x8 -> x0, waiting for transfers between devices: 73 us -> none  [one_exchange(): lax.all_to_all(pieces, axis, split_axis=0, concat_axis=0, tiled=True)]
    all_to_all x8 -> x0, starting transfers between devices: 62.8 us -> none  [one_exchange(): lax.all_to_all(pieces, axis, split_axis=0, concat_axis=0, tiled=True)]
    dot_general x21 -> x0, matrix products: 26.3 us -> none  [the longest x4 13.5 us: shards(): jnp.einsum('krb,kbc->krc', picked, off_blocks[level_at], preferred_elemen...]
    pallas_call x0 -> x5, Pallas kernels: none -> 17.6 us  [the longest x4 12.7 us: shards(): pl.pallas_call(functools.partial(later_kernel, level, levels), out_shape=...]
    dot_general x4 -> x0, local copies, waits for them, and re-layouts: 7.2 us -> none  [shards(): jnp.dot(packer.astype(jnp.float32), contribution, precision=lax.Precision...]
    lt x5 -> x0, other arithmetic: 3.15 us -> none  [shards(): slot_ids < live_counts[level_at, 0]]
    sub x4 -> x0, local copies, waits for them, and re-layouts: 3.08 us -> none  [shards(): jnp.sum(packer.astype(jnp.int32) * (blocks_now + 1)[None, :], axis=1) - 1]
  transfers between devices with their start and end apart: 8 -> 0, of which waited for: 7 -> 0; matrix products, arithmetic and copies ran while one was open for 23% -> 0% of each run, Pallas kernels for 0% -> 0%
where the time goes in v2:
time: 120 us; the launch traced here: 119 us
  blocking collectives  102 us (85%)
  Pallas kernels  17.6 us (15%)
    all_to_all x3, blocking collectives, shards(): arrived = lax.all_to_all(outgoing, AXES, 0, 0, tiled=True)  70.6 us
    all_to_all x1, blocking collectives, shards(): lax.all_to_all(outgoing, AXES, 0, 0, tiled=True)  31.2 us
    pallas_call x4, Pallas kernels, shards(): pl.pallas_call(functools.partial(later_kernel, level, levels), out_shape=...  12.7 us
    pallas_call x1, Pallas kernels, shards(): pl.pallas_call(functools.partial(first_kernel, dummy), out_shape=[solved_...  4.88 us

profile of v2, /device:TPU:1, one launch (start us, length us, event | category | flops | bytes accessed | tf_op | source)
XLA Modules:
  0.0 119.4 jit_solution(13568679120006425928)
XLA Ops:
  0.0 4.9 %level_0.1 = (f32[16,8,128]{2,1,0:T(8,128)S(1)}, f32[2176,128]{1,0:T(8,128)S(1)}, s32[4,128]{1,0:T(4,128)S(1)}, s32[1,5]{1,0:T(1,128)S(1)}, s32[4,128]{1,0:T(4,1...) custom-call(s32[1,5]{1,0:T(1,128)} %bitcast.17, ...), custom_call_target="tpu_custom_call" | custom-call | tf_op jit(solution)/shard_map/level_0/pallas_call | solution.py:216
  4.9 31.2 %all_to_all.20 = f32[128,17,1,128]{3,2,1,0:T(1,128)S(1)} all-to-all(f32[128,17,1,128]{3,2,1,0:T(1,128)S(1)} %bitcast.13), channel_id=1, replica_groups=mesh['gx'=4,'gy'=4,'gz'=8] {'gx','gy','gz'}, dimensions={0} | all-to-all | bytes 2228224 | tf_op jit(solution)/shard_map/all_to_all | solution.py:245
  36.0 3.6 %level_1.1 = (f32[16,8,128]{2,1,0:T(8,128)S(1)}, f32[256,8,128]{2,1,0:T(8,128)S(1)}, f32[81,8,128]{2,1,0:T(8,128)S(1)}, f32[81,8,128]{2,1,0:T(8,128)S(1)}, f32[8...) custom-call(s32[1,5]{1,0:T(1,128)S(1)} %get-tuple-element.33.refs_0_, ...), custom_call_target="tpu_custom_call", output_to_operand_aliasing={{2}: (2, {}), {3}: (3, {}), {4}: (4, {}), {5}: (5, {})} | custom-call | tf_op jit(solution)/shard_map/level_1/pallas_call | solution.py:281
  39.6 23.5 %all_to_all.21 = f32[128,16,128]{2,1,0:T(8,128)S(1)} all-to-all(f32[128,16,128]{2,1,0:T(8,128)S(1)} %bitcast.15), channel_id=1, replica_groups=mesh['gx'=4,'gy'=4,'gz'=8] {'gx','gy','gz'}, dimensions={0} | all-to-all | bytes 2097152 | tf_op jit(solution)/shard_map/all_to_all | solution.py:299
  63.1 3.5 %level_2.1 = (f32[16,8,128]{2,1,0:T(8,128)S(1)}, f32[256,8,128]{2,1,0:T(8,128)S(1)}, f32[81,8,128]{2,1,0:T(8,128)S(1)}, f32[81,8,128]{2,1,0:T(8,128)S(1)}, f32[8...) custom-call(s32[1,5]{1,0:T(1,128)S(1)} %get-tuple-element.33.refs_0_, ...), custom_call_target="tpu_custom_call", output_to_operand_aliasing={{2}: (2, {}), {3}: (3, {}), {4}: (4, {}), {5}: (5, {})} | custom-call | tf_op jit(solution)/shard_map/level_2/pallas_call | solution.py:281
  66.6 23.5 %all_to_all.22 = f32[128,16,128]{2,1,0:T(8,128)S(1)} all-to-all(f32[128,16,128]{2,1,0:T(8,128)S(1)} %bitcast.16), channel_id=1, replica_groups=mesh['gx'=4,'gy'=4,'gz'=8] {'gx','gy','gz'}, dimensions={0} | all-to-all | bytes 2097152 | tf_op jit(solution)/shard_map/all_to_all | solution.py:299
  90.2 3.5 %level_3.1 = (f32[16,8,128]{2,1,0:T(8,128)S(1)}, f32[256,8,128]{2,1,0:T(8,128)S(1)}, f32[81,8,128]{2,1,0:T(8,128)S(1)}, f32[81,8,128]{2,1,0:T(8,128)S(1)}, f32[8...) custom-call(s32[1,5]{1,0:T(1,128)S(1)} %get-tuple-element.33.refs_0_, ...), custom_call_target="tpu_custom_call", output_to_operand_aliasing={{2}: (2, {}), {3}: (3, {}), {4}: (4, {}), {5}: (5, {})} | custom-call | tf_op jit(solution)/shard_map/level_3/pallas_call | solution.py:281
  93.7 23.5 %all_to_all.23 = f32[128,16,128]{2,1,0:T(8,128)S(1)} all-to-all(f32[128,16,128]{2,1,0:T(8,128)S(1)} %bitcast.14), channel_id=1, replica_groups=mesh['gx'=4,'gy'=4,'gz'=8] {'gx','gy','gz'}, dimensions={0} | all-to-all | bytes 2097152 | tf_op jit(solution)/shard_map/all_to_all | solution.py:299
  117.3 2.1 %level_4.1 = f32[5,16,8,128]{3,2,1,0:T(8,128)} custom-call(s32[1,5]{1,0:T(1,128)S(1)} %get-tuple-element.33.refs_0_, f32[2048,128]{1,0:T(8,128)S(1)} %bitcast.12, f32[81,8,128]{2,1,0:T(8,128)S(1)} %get-tuple-element.53.refs_2_, f32[81,8,128]{2,1,0:T(8,128)S(1)} %get-tuple-element.54.refs_3_, f32[81,8,128]{2,1,0:T(8,128)S(1)} %get-tuple-element.55.refs_4_, ...), custom_call_target="tpu_custom_call" | custom-call | tf_op jit(solution)/shard_map/level_4/pallas_call | solution.py:281

commit v3 on v2

v3 whole, which is shorter than its diff:
```python
import functools

import jax
import jax.numpy as jnp
from jax import lax
from jax.experimental import pallas as pl
from jax.experimental.pallas import tpu as pltpu
from jax.sharding import PartitionSpec as P

CAP = 2
CHAINS = 4
CHUNKS = 2
AXES = ("gx", "gy", "gz")
VMEM = pl.BlockSpec(memory_space=pltpu.VMEM)
HBM = pl.BlockSpec(memory_space=pltpu.HBM)
CONTRACT_LANES = (((1,), (1,)), ((), ()))


def solve(level, rhs, diag, counts, accs, solved):
    slots = solved.shape[0]
    live = jnp.broadcast_to(counts[:, level : level + 1], solved.shape[1:])
    for slot in range(slots):
        work = rhs[slot]
        if accs:
            at = level * slots + slot
            work = work - ((accs[0][at] + accs[1][at]) + (accs[2][at] + accs[3][at]))
        value = jnp.dot(work.astype(jnp.bfloat16), diag[slot], preferred_element_type=jnp.float32)
        solved[slot] = jnp.where(live > slot, value, jnp.float32(0.0))


class Level:
    def __init__(self, level, sems, pairs, off_hbm=None, off=None, begin=0, chunks=CHUNKS):
        self.parts = [
            pltpu.make_async_copy(source.at[level], held, sems.at[CHUNKS + at])
            for at, (source, held) in enumerate(pairs)
        ]
        self.chunks = []
        self.begin = begin
        if off is not None:
            self.span = off.shape[0] // chunks

            def chunk_copy(chunk):
                rows = pl.ds(chunk * self.span, self.span)
                rows_hbm = pl.ds(begin + chunk * self.span, self.span)
                return pltpu.make_async_copy(
                    off_hbm.at[level, rows_hbm], off.at[rows], sems.at[chunk]
                )

            self.chunk_copy = chunk_copy
            self.chunks = [chunk_copy(chunk) for chunk in range(chunks)]
        for copy in self.parts + self.chunks:
            copy.start()

    def wait_parts(self):
        for copy in self.parts:
            copy.wait()

    def wait_chunk(self, chunk):
        self.chunk_copy(chunk).wait()

    def wait_record(self, record):
        if record >= self.begin and (record - self.begin) % self.span == 0:
            self.chunks[(record - self.begin) // self.span].wait()

    def wait(self):
        for copy in self.parts + self.chunks:
            copy.wait()


def clear(filled):
    for at in range(filled.shape[0]):
        filled[at] = 0


def contribute(loaded, off_of, solved, scalars, filled, level, outgoing, stride, group=None):
    height = solved.shape[1]
    source, owner = scalars

    def one(record):
        picked = solved[source[level, record]].astype(jnp.bfloat16)
        value = jnp.dot(picked, off_of(record), preferred_element_type=jnp.float32)
        to = owner[level, record]
        place = filled[to]
        filled[to] = place + 1
        row = to * stride + place * height
        if stride % height == 0:
            row = pl.multiple_of(row, height)
        outgoing[pl.ds(row, height), :] = value

    records = source.shape[1]
    if group is None:
        for record in range(records):
            if loaded is not None:
                loaded.wait_record(record)
            one(record)
        return

    def several(at, carry):
        if loaded is not None:
            loaded.wait_chunk(at)
        for record in range(group):
            one(at * group + record)
        return carry

    lax.fori_loop(0, records // group, several, 0)


def first_kernel(
    dummy, counts_hbm, source_hbm, owner_hbm, block_hbm, rhs_hbm, diag_hbm, off_hbm,
    solved, outgoing, counts, source, owner, acc_0, acc_1, acc_2, acc_3,
    next_rhs, next_diag, next_off,
    rhs, diag, off, block, source_smem, owner_smem, filled, table_sems, sems, next_sems,
):
    tables = (
        (owner_hbm, owner),
        (block_hbm, block),
        (counts_hbm, counts),
        (source_hbm, source),
        (source_hbm, source_smem),
        (owner_hbm, owner_smem),
    )
    tables = [
        pltpu.make_async_copy(table, held, table_sems.at[at])
        for at, (table, held) in enumerate(tables)
    ]
    for copy in tables:
        copy.start()
    loaded = Level(0, sems, ((rhs_hbm, rhs), (diag_hbm, diag)), off_hbm, off)
    coming = Level(
        1, next_sems, ((rhs_hbm, next_rhs), (diag_hbm, next_diag)), off_hbm, next_off, 0, 1
    )
    clear(filled)
    for acc in (acc_0, acc_1, acc_2, acc_3):
        for row in range(acc.shape[0]):
            acc[row] = jnp.zeros(acc.shape[1:], jnp.float32)
    exchanges, width = owner.shape
    owners = width
    stride = outgoing.shape[0] // owners
    height = solved.shape[1]
    for copy in tables:
        copy.wait()
    loaded.wait_parts()
    solve(0, rhs, diag, counts, None, solved)
    down = lax.broadcasted_iota(jnp.int32, (owners, width), 0)
    along = lax.broadcasted_iota(jnp.int32, (owners, width), 1)
    before = (down < along).astype(jnp.bfloat16)
    labels = jnp.full((owners, width), dummy, jnp.float32)
    for level in range(exchanges):
        hit = (down == owner[level : level + 1, :]).astype(jnp.float32)
        hit_low = hit.astype(jnp.bfloat16)
        earlier = jnp.dot(hit_low, before, preferred_element_type=jnp.float32)
        position = jnp.sum(hit * earlier, axis=0, keepdims=True)
        value = (block[level : level + 1, :] - dummy).astype(jnp.float32)
        spread = jnp.where(
            down == CAP * level,
            value * (1.0 - position),
            jnp.where(down == CAP * level + 1, value * position, 0.0),
        ).astype(jnp.bfloat16)
        labels = labels + lax.dot_general(
            hit_low, spread, CONTRACT_LANES, preferred_element_type=jnp.float32
        )
    outgoing[pl.ds(CAP * height, owners, stride=stride), :] = labels
    off_of = lambda record: off[record]
    contribute(loaded, off_of, solved, (source_smem, owner_smem), filled, 0, outgoing, stride, 64)
    coming.wait()


def later_kernel(level, levels, *refs):
    last = level == levels - 1
    more = level < levels - 2
    refs = list(refs)
    take = lambda count: [refs.pop(0) for _ in range(count)]
    counts, arrived = take(2)
    accs = take(CHAINS)
    label_table = take(1)[0] if level > 1 else None
    rhs, diag = take(2)
    off_hbm = next_off = None
    if not last:
        source, owner, off, rhs_hbm, diag_hbm = take(5)
        if more:
            off_hbm = take(1)[0]
        solved, outgoing = take(2)
        accs = take(CHAINS)
        next_rhs, next_diag = take(2)
        if more:
            next_off = take(1)[0]
        if level == 1:
            label_table, off_rest, rest_sems = take(3)
        source_smem, owner_smem, filled, next_sems = take(4)
    else:
        earlier = take(level)
        result, solved = take(2)
    label_smem, table_sems = refs
    height, width = solved.shape[1:]
    owners = label_smem.shape[1]
    stride = arrived.shape[0] // owners
    rest = None
    if level == 1:
        begin = off.shape[0]
        rest = Level(level, rest_sems, (), off_hbm, off_rest, begin, 2)
        rows = arrived[pl.ds(CAP * height, owners, stride=stride), :].astype(jnp.bfloat16)
        down = lax.broadcasted_iota(jnp.int32, (label_table.shape[0], width), 0)
        along = lax.broadcasted_iota(jnp.int32, (label_table.shape[0], width), 1)
        turned = lax.dot_general(
            (down == along).astype(jnp.bfloat16),
            rows,
            CONTRACT_LANES,
            preferred_element_type=jnp.float32,
        )
        label_table[...] = turned.astype(jnp.int32)
    label_copy = pltpu.make_async_copy(label_table, label_smem, table_sems.at[0])
    label_copy.start()
    copies = []
    if not last:
        for at, (table, scalars) in enumerate(((source, source_smem), (owner, owner_smem))):
            copies.append(pltpu.make_async_copy(table, scalars, table_sems.at[1 + at]))
    else:
        for at, piece in enumerate(earlier):
            copies.append(pltpu.make_async_copy(piece, result.at[at], table_sems.at[1 + at]))
    for copy in copies:
        copy.start()
    if not last:
        coming = Level(
            level + 1,
            next_sems,
            ((rhs_hbm, next_rhs), (diag_hbm, next_diag)),
            off_hbm,
            next_off,
            0,
            1,
        )
        clear(filled)
    label_copy.wait()
    for sender in range(owners):
        for place in range(CAP):
            acc = accs[(sender % 2) * CAP + place]
            row = label_smem[CAP * (level - 1) + place, sender]
            at = sender * stride + place * height
            acc[row] = acc[row] + arrived[at : at + height, :]
    solve(level, rhs, diag, counts, accs, solved)
    if last:
        copy = pltpu.make_async_copy(solved, result.at[level], table_sems.at[1 + level])
        copy.start()
        copies.append(copy)
    for copy in copies:
        copy.wait()
    if not last:
        scalars = (source_smem, owner_smem)
        if rest is None:
            off_of = lambda record: off[record]
        else:
            off_of = lambda record: off[record] if record < begin else off_rest[record - begin]
        contribute(rest, off_of, solved, scalars, filled, level, outgoing, CAP * height)
        coming.wait()


def shards(
    right_side, diag_inverse, off_blocks, live_counts, source_slot, target_owner, target_block
):
    levels, slots, height, width = right_side.shape
    exchanges, records = off_blocks.shape[:2]
    owners = lax.axis_size(AXES)
    dummy = levels * slots
    counts = live_counts.T
    stride = CAP * height + 1
    in_hbm = lambda x: pltpu.with_memory_space_constraint(x, pltpu.HBM)
    right_side, diag_inverse, off_blocks = map(in_hbm, (right_side, diag_inverse, off_blocks))
    tables = list(map(in_hbm, (counts, source_slot, target_owner, target_block)))
    table_shape = pltpu.VMEM((exchanges, records), jnp.int32)
    params = pltpu.CompilerParams(vmem_limit_bytes=24 * 1024 * 1024)
    acc_shapes = [pltpu.VMEM((dummy + 1, height, width), jnp.float32)] * CHAINS
    solved_shape = pltpu.VMEM((slots, height, width), jnp.float32)
    level_shapes = [
        pltpu.VMEM((slots, height, width), jnp.float32),
        pltpu.VMEM((slots, width, width), jnp.bfloat16),
        pltpu.VMEM((records, width, width), jnp.bfloat16),
    ]
    half_shape = pltpu.VMEM((records // 2, width, width), jnp.bfloat16)
    filled_scratch = pltpu.SMEM((owners,), jnp.int32)
    table_scratch = pltpu.SMEM((exchanges, records), jnp.int32)
    level_sems = pltpu.SemaphoreType.DMA((2 + CHUNKS,))
    out = pl.pallas_call(
        functools.partial(first_kernel, dummy),
        out_shape=[
            solved_shape,
            pltpu.VMEM((owners * stride, width), jnp.float32),
            pltpu.VMEM(counts.shape, jnp.int32),
            table_shape,
            table_shape,
            *acc_shapes,
            *level_shapes[:2],
            half_shape,
        ],
        in_specs=[HBM] * 7,
        out_specs=[VMEM] * (8 + CHAINS),
        scratch_shapes=[
            *level_shapes,
            table_shape,
            table_scratch,
            table_scratch,
            filled_scratch,
            pltpu.SemaphoreType.DMA((6,)),
            level_sems,
            level_sems,
        ],
        compiler_params=params,
        name="level_0",
    )(*tables, right_side, diag_inverse, off_blocks)
    solved, outgoing, counts, source_slot, target_owner = out[:5]
    accs = out[5 : 5 + CHAINS]
    held = out[5 + CHAINS :]
    outgoing = outgoing.reshape(owners, stride, 1, width)
    arrived = lax.all_to_all(outgoing, AXES, 0, 0, tiled=True).reshape(owners * stride, width)
    results = [solved]
    label_table = None
    label_shape = (CAP * exchanges, owners)
    for level in range(1, levels):
        last = level == levels - 1
        args = [counts, arrived, *accs]
        specs = [VMEM] * (2 + CHAINS)
        if level > 1:
            args += [label_table]
            specs += [VMEM]
        args += held[:2]
        specs += [VMEM] * 2
        tail = [pltpu.SMEM(label_shape, jnp.int32)]
        aliases = {}
        if not last:
            more = 3 if level < levels - 2 else 2
            args += [source_slot, target_owner, held[2]]
            args += [right_side, diag_inverse, off_blocks][:more]
            specs += [VMEM] * 3 + [HBM] * more
            shapes = [
                solved_shape,
                pltpu.VMEM((owners * CAP * height, width), jnp.float32),
                *acc_shapes,
                *level_shapes[:more],
            ]
            aliases = {2 + chain: 2 + chain for chain in range(CHAINS)}
            if level == 1:
                shapes += [pltpu.VMEM(label_shape, jnp.int32)]
            out_specs = [VMEM] * len(shapes)
            scratch = [table_scratch, table_scratch, filled_scratch, level_sems] + tail
            if level == 1:
                scratch = [half_shape, level_sems] + scratch
            scratch += [pltpu.SemaphoreType.DMA((3,))]
        else:
            args += results
            specs += [VMEM] * level
            shapes = jax.ShapeDtypeStruct((levels, slots, height, width), jnp.float32)
            out_specs = HBM
            scratch = [pltpu.VMEM((slots, height, width), jnp.float32)] + tail
            scratch += [pltpu.SemaphoreType.DMA((2 + level,))]
        out = pl.pallas_call(
            functools.partial(later_kernel, level, levels),
            out_shape=shapes,
            in_specs=specs,
            out_specs=out_specs,
            scratch_shapes=scratch,
            input_output_aliases=aliases,
            compiler_params=params,
            name=f"level_{level}",
        )(*args)
        if last:
            return out
        solved, outgoing = out[:2]
        accs = out[2 : 2 + CHAINS]
        held = out[2 + CHAINS : 2 + CHAINS + more]
        if level == 1:
            label_table = out[2 + CHAINS + more]
        results.append(solved)
        outgoing = outgoing.reshape(owners, CAP * height, width)
        arrived = lax.all_to_all(outgoing, AXES, 0, 0, tiled=True)
        arrived = arrived.reshape(owners * CAP * height, width)


def solution(mesh):
    split = P(None, AXES, None, None)
    flat = P(None, AXES)
    return jax.shard_map(
        shards,
        mesh=mesh,
        in_specs=(split, split, split, flat, flat, flat, flat),
        out_specs=split,
        check_vma=False,
    )
```

time: 120 us -> 116 us (0.967)
  Pallas kernels: 17.6 us -> 13.5 us
    pallas_call x4, Pallas kernels: 12.7 us -> 10.1 us  [shards(): pl.pallas_call(functools.partial(later_kernel, level, levels), out_shape=...]
    pallas_call x1, Pallas kernels: 4.88 us -> 3.46 us  [shards(): pl.pallas_call(functools.partial(first_kernel, dummy), out_shape=[solved_...]
where the time goes in v3:
time: 116 us; the launch traced here: 115 us
  blocking collectives  102 us (88%)
  Pallas kernels  13.5 us (12%)
    all_to_all x3, blocking collectives, shards(): arrived = lax.all_to_all(outgoing, AXES, 0, 0, tiled=True)  70.7 us
    all_to_all x1, blocking collectives, shards(): lax.all_to_all(outgoing, AXES, 0, 0, tiled=True)  31.2 us
    pallas_call x4, Pallas kernels, shards(): pl.pallas_call(functools.partial(later_kernel, level, levels), out_shape=...  10.1 us
    pallas_call x1, Pallas kernels, shards(): pl.pallas_call(functools.partial(first_kernel, dummy), out_shape=[solved_...  3.46 us

profile of v3, /device:TPU:1, one launch (start us, length us, event | category | flops | bytes accessed | tf_op | source)
XLA Modules:
  0.0 115.4 jit_solution(3063898781392090860)
XLA Ops:
  0.0 3.5 %level_0.1 = (f32[16,8,128]{2,1,0:T(8,128)S(1)}, f32[2176,128]{1,0:T(8,128)S(1)}, s32[1,5]{1,0:T(1,128)S(1)}, s32[4,128]{1,0:T(4,128)S(1)}, s32[4,128]{1,0:T(4,1...) custom-call(s32[1,5]{1,0:T(1,128)} %bitcast.17, ...), custom_call_target="tpu_custom_call" | custom-call | tf_op jit(solution)/shard_map/level_0/pallas_call | solution.py:282
  3.5 31.2 %all_to_all.20 = f32[128,17,1,128]{3,2,1,0:T(1,128)S(1)} all-to-all(f32[128,17,1,128]{3,2,1,0:T(1,128)S(1)} %bitcast.13), channel_id=1, replica_groups=mesh['gx'=4,'gy'=4,'gz'=8] {'gx','gy','gz'}, dimensions={0} | all-to-all | bytes 2228224 | tf_op jit(solution)/shard_map/all_to_all | solution.py:313
  34.6 3.1 %level_1.1 = (f32[16,8,128]{2,1,0:T(8,128)S(1)}, f32[2048,128]{1,0:T(8,128)S(1)}, f32[81,8,128]{2,1,0:T(8,128)S(1)}, f32[81,8,128]{2,1,0:T(8,128)S(1)}, f32[81,8...) custom-call(s32[1,5]{1,0:T(1,128)S(1)} %get-tuple-element.44.refs_0_, ...), custom_call_target="tpu_custom_call", output_to_operand_aliasing={{2}: (2, {}), {3}: (3, {}), {4}: (4, {}), {5}: (5, {})} | custom-call | tf_op jit(solution)/shard_map/level_1/pallas_call | solution.py:354
  37.8 23.6 %all_to_all.21 = f32[128,16,128]{2,1,0:T(8,128)S(1)} all-to-all(f32[128,16,128]{2,1,0:T(8,128)S(1)} %bitcast.14), channel_id=1, replica_groups=mesh['gx'=4,'gy'=4,'gz'=8] {'gx','gy','gz'}, dimensions={0} | all-to-all | bytes 2097152 | tf_op jit(solution)/shard_map/all_to_all | solution.py:373
  61.3 2.5 %level_2.1 = (f32[16,8,128]{2,1,0:T(8,128)S(1)}, f32[2048,128]{1,0:T(8,128)S(1)}, f32[81,8,128]{2,1,0:T(8,128)S(1)}, f32[81,8,128]{2,1,0:T(8,128)S(1)}, f32[81,8...) custom-call(s32[1,5]{1,0:T(1,128)S(1)} %get-tuple-element.44.refs_0_, ...), custom_call_target="tpu_custom_call", output_to_operand_aliasing={{2}: (2, {}), {3}: (3, {}), {4}: (4, {}), {5}: (5, {})} | custom-call | tf_op jit(solution)/shard_map/level_2/pallas_call | solution.py:354
  63.9 23.6 %all_to_all.22 = f32[128,16,128]{2,1,0:T(8,128)S(1)} all-to-all(f32[128,16,128]{2,1,0:T(8,128)S(1)} %bitcast.16), channel_id=1, replica_groups=mesh['gx'=4,'gy'=4,'gz'=8] {'gx','gy','gz'}, dimensions={0} | all-to-all | bytes 2097152 | tf_op jit(solution)/shard_map/all_to_all | solution.py:373
  87.4 2.5 %level_3.1 = (f32[16,8,128]{2,1,0:T(8,128)S(1)}, f32[2048,128]{1,0:T(8,128)S(1)}, f32[81,8,128]{2,1,0:T(8,128)S(1)}, f32[81,8,128]{2,1,0:T(8,128)S(1)}, f32[81,8...) custom-call(s32[1,5]{1,0:T(1,128)S(1)} %get-tuple-element.44.refs_0_, ...), custom_call_target="tpu_custom_call", output_to_operand_aliasing={{2}: (2, {}), {3}: (3, {}), {4}: (4, {}), {5}: (5, {})} | custom-call | tf_op jit(solution)/shard_map/level_3/pallas_call | solution.py:354
  90.0 23.6 %all_to_all.23 = f32[128,16,128]{2,1,0:T(8,128)S(1)} all-to-all(f32[128,16,128]{2,1,0:T(8,128)S(1)} %bitcast.15), channel_id=1, replica_groups=mesh['gx'=4,'gy'=4,'gz'=8] {'gx','gy','gz'}, dimensions={0} | all-to-all | bytes 2097152 | tf_op jit(solution)/shard_map/all_to_all | solution.py:373
  113.5 1.9 %level_4.1 = f32[5,16,8,128]{3,2,1,0:T(8,128)} custom-call(s32[1,5]{1,0:T(1,128)S(1)} %get-tuple-element.44.refs_0_, f32[2048,128]{1,0:T(8,128)S(1)} %bitcast.12, f32[81,8,128]{2,1,0:T(8,128)S(1)} %get-tuple-element.73.refs_2_, f32[81,8,128]{2,1,0:T(8,128)S(1)} %get-tuple-element.74.refs_3_, f32[81,8,128]{2,1,0:T(8,128)S(1)} %get-tuple-element.75.refs_4_, ...), custom_call_target="tpu_custom_call" | custom-call | tf_op jit(solution)/shard_map/level_4/pallas_call | solution.py:354

commit v4 on v3

--- a/solution.py
+++ b/solution.py
@@ -16,7 +16,7 @@
 CONTRACT_LANES = (((1,), (1,)), ((), ()))
 
 
-def solve(level, rhs, diag, counts, accs, solved):
+def solve(level, rhs, diag, counts, accs, fresh, solved):
     slots = solved.shape[0]
     live = jnp.broadcast_to(counts[:, level : level + 1], solved.shape[1:])
     for slot in range(slots):
@@ -24,6 +24,9 @@
         if accs:
             at = level * slots + slot
             work = work - ((accs[0][at] + accs[1][at]) + (accs[2][at] + accs[3][at]))
+        if fresh is not None:
+            height = rhs.shape[1]
+            work = work - fresh[slot * height : (slot + 1) * height, :]
         value = jnp.dot(work.astype(jnp.bfloat16), diag[slot], preferred_element_type=jnp.float32)
         solved[slot] = jnp.where(live > slot, value, jnp.float32(0.0))
 
@@ -72,7 +75,27 @@
         filled[at] = 0
 
 
-def contribute(loaded, off_of, solved, scalars, filled, level, outgoing, stride, group=None):
+def gather_fresh(level, labels, arrived, stride, height, fresh):
+    slots = fresh.shape[0] // height
+    owners = labels[0].shape[1]
+    down = lax.broadcasted_iota(jnp.int32, (slots, owners), 0) + level * slots
+    hits = jnp.concatenate([(down == row).astype(jnp.bfloat16) for row in labels], axis=1)
+    for row in range(height):
+        values = jnp.concatenate(
+            [
+                arrived[pl.ds(place * height + row, owners, stride=stride), :]
+                for place in range(CAP)
+            ],
+            axis=0,
+        )
+        high = values.astype(jnp.bfloat16)
+        low = (values - high.astype(jnp.float32)).astype(jnp.bfloat16)
+        fresh[pl.ds(row, slots, stride=height), :] = jnp.dot(
+            hits, high, preferred_element_type=jnp.float32
+        ) + jnp.dot(hits, low, preferred_element_type=jnp.float32)
+
+
+def contribute(loaded, off_of, solved, scalars, filled, level, outgoing, stride, group, beside):
     height = solved.shape[1]
     source, owner = scalars
 
@@ -86,6 +109,8 @@
         if stride % height == 0:
             row = pl.multiple_of(row, height)
         outgoing[pl.ds(row, height), :] = value
+        if beside is not None:
+            beside(record)
 
     records = source.shape[1]
     if group is None:
@@ -105,11 +130,17 @@
     lax.fori_loop(0, records // group, several, 0)
 
 
+def clear_rows(outgoing, stride, height, owners):
+    for owner in range(owners):
+        for place in range(CAP):
+            at = owner * stride + place * height
+            outgoing[at : at + height, :] = jnp.zeros((height, outgoing.shape[1]), jnp.float32)
+
+
 def first_kernel(
     dummy, counts_hbm, source_hbm, owner_hbm, block_hbm, rhs_hbm, diag_hbm, off_hbm,
-    solved, outgoing, counts, source, owner, acc_0, acc_1, acc_2, acc_3,
-    next_rhs, next_diag, next_off,
-    rhs, diag, off, block, source_smem, owner_smem, filled, table_sems, sems, next_sems,
+    solved, outgoing, counts, source, owner,
+    rhs, diag, off, block, source_smem, owner_smem, filled, table_sems, sems,
 ):
     tables = (
         (owner_hbm, owner),
@@ -126,21 +157,16 @@
     for copy in tables:
         copy.start()
     loaded = Level(0, sems, ((rhs_hbm, rhs), (diag_hbm, diag)), off_hbm, off)
-    coming = Level(
-        1, next_sems, ((rhs_hbm, next_rhs), (diag_hbm, next_diag)), off_hbm, next_off, 0, 1
-    )
     clear(filled)
-    for acc in (acc_0, acc_1, acc_2, acc_3):
-        for row in range(acc.shape[0]):
-            acc[row] = jnp.zeros(acc.shape[1:], jnp.float32)
     exchanges, width = owner.shape
     owners = width
     stride = outgoing.shape[0] // owners
     height = solved.shape[1]
+    clear_rows(outgoing, stride, height, owners)
     for copy in tables:
         copy.wait()
     loaded.wait_parts()
-    solve(0, rhs, diag, counts, None, solved)
+    solve(0, rhs, diag, counts, None, None, solved)
     down = lax.broadcasted_iota(jnp.int32, (owners, width), 0)
     along = lax.broadcasted_iota(jnp.int32, (owners, width), 1)
     before = (down < along).astype(jnp.bfloat16)
@@ -161,43 +187,45 @@
         )
     outgoing[pl.ds(CAP * height, owners, stride=stride), :] = labels
     off_of = lambda record: off[record]
-    contribute(loaded, off_of, solved, (source_smem, owner_smem), filled, 0, outgoing, stride, 64)
-    coming.wait()
+    contribute(loaded, off_of, solved, (source_smem, owner_smem), filled, 0, outgoing, stride, 64, None)
 
 
 def later_kernel(level, levels, *refs):
     last = level == levels - 1
-    more = level < levels - 2
     refs = list(refs)
     take = lambda count: [refs.pop(0) for _ in range(count)]
     counts, arrived = take(2)
-    accs = take(CHAINS)
+    accs = take(CHAINS) if level > 1 else []
     label_table = take(1)[0] if level > 1 else None
     rhs, diag = take(2)
-    off_hbm = next_off = None
     if not last:
-        source, owner, off, rhs_hbm, diag_hbm = take(5)
-        if more:
-            off_hbm = take(1)[0]
-        solved, outgoing = take(2)
-        accs = take(CHAINS)
-        next_rhs, next_diag = take(2)
-        if more:
-            next_off = take(1)[0]
+        source, owner, off, solved, outgoing = take(5)
+        next_accs = take(CHAINS)
         if level == 1:
-            label_table, off_rest, rest_sems = take(3)
-        source_smem, owner_smem, filled, next_sems = take(4)
+            label_table = take(1)[0]
+        source_smem, owner_smem, label_smem, filled = take(4)
     else:
         earlier = take(level)
         result, solved = take(2)
-    label_smem, table_sems = refs
+    fresh, fence, table_sems = refs
     height, width = solved.shape[1:]
-    owners = label_smem.shape[1]
+    owners = width
     stride = arrived.shape[0] // owners
-    rest = None
+    if not last:
+        tables = [(source, source_smem), (owner, owner_smem)]
+        if level > 1:
+            tables += [(label_table, label_smem)]
+    else:
+        tables = [(piece, result.at[at]) for at, piece in enumerate(earlier)]
+    copies = [
+        pltpu.make_async_copy(table, held, table_sems.at[at])
+        for at, (table, held) in enumerate(tables)
+    ]
+    for copy in copies:
+        copy.start()
+    pl.semaphore_signal(fence, 1)
+    pl.semaphore_wait(fence, 1)
     if level == 1:
-        begin = off.shape[0]
-        rest = Level(level, rest_sems, (), off_hbm, off_rest, begin, 2)
         rows = arrived[pl.ds(CAP * height, owners, stride=stride), :].astype(jnp.bfloat16)
         down = lax.broadcasted_iota(jnp.int32, (label_table.shape[0], width), 0)
         along = lax.broadcasted_iota(jnp.int32, (label_table.shape[0], width), 1)
@@ -208,50 +236,42 @@
             preferred_element_type=jnp.float32,
         )
         label_table[...] = turned.astype(jnp.int32)
-    label_copy = pltpu.make_async_copy(label_table, label_smem, table_sems.at[0])
-    label_copy.start()
-    copies = []
+        label_copy = pltpu.make_async_copy(label_table, label_smem, table_sems.at[2])
+        label_copy.start()
+        copies.append(label_copy)
     if not last:
-        for at, (table, scalars) in enumerate(((source, source_smem), (owner, owner_smem))):
-            copies.append(pltpu.make_async_copy(table, scalars, table_sems.at[1 + at]))
-    else:
-        for at, piece in enumerate(earlier):
-            copies.append(pltpu.make_async_copy(piece, result.at[at], table_sems.at[1 + at]))
+        clear(filled)
+        clear_rows(outgoing, CAP * height, height, owners)
+    first_label = CAP * (level - 1)
+    labels = [label_table[first_label + place : first_label + place + 1, :] for place in range(CAP)]
+    gather_fresh(level, labels, arrived, stride, height, fresh)
+    solve(level, rhs.at[level], diag.at[level], counts, accs, fresh, solved)
+    if last:
+        copy = pltpu.make_async_copy(solved, result.at[level], table_sems.at[level])
+        copy.start()
+        copies.append(copy)
+        for copy in copies:
+            copy.wait()
+        return
+    if level == 1:
+        for acc in next_accs:
+            for row in range((level + 1) * solved.shape[0], acc.shape[0]):
+                acc[row] = jnp.zeros(acc.shape[1:], jnp.float32)
     for copy in copies:
-        copy.start()
-    if not last:
-        coming = Level(
-            level + 1,
-            next_sems,
-            ((rhs_hbm, next_rhs), (diag_hbm, next_diag)),
-            off_hbm,
-            next_off,
-            0,
-            1,
-        )
-        clear(filled)
-    label_copy.wait()
-    for sender in range(owners):
+        copy.wait()
+
+    def accumulate(sender):
         for place in range(CAP):
-            acc = accs[(sender % 2) * CAP + place]
-            row = label_smem[CAP * (level - 1) + place, sender]
+            acc = next_accs[(sender % 2) * CAP + place]
+            row = label_smem[first_label + place, sender]
             at = sender * stride + place * height
             acc[row] = acc[row] + arrived[at : at + height, :]
-    solve(level, rhs, diag, counts, accs, solved)
-    if last:
-        copy = pltpu.make_async_copy(solved, result.at[level], table_sems.at[1 + level])
-        copy.start()
-        copies.append(copy)
-    for copy in copies:
-        copy.wait()
-    if not last:
-        scalars = (source_smem, owner_smem)
-        if rest is None:
-            off_of = lambda record: off[record]
-        else:
-            off_of = lambda record: off[record] if record < begin else off_rest[record - begin]
-        contribute(rest, off_of, solved, scalars, filled, level, outgoing, CAP * height)
-        coming.wait()
+
+    off_of = lambda record: off[level, record]
+    scalars = (source_smem, owner_smem)
+    contribute(
+        None, off_of, solved, scalars, filled, level, outgoing, CAP * height, None, accumulate
+    )
 
 
 def shards(
@@ -264,7 +284,6 @@
     counts = live_counts.T
     stride = CAP * height + 1
     in_hbm = lambda x: pltpu.with_memory_space_constraint(x, pltpu.HBM)
-    right_side, diag_inverse, off_blocks = map(in_hbm, (right_side, diag_inverse, off_blocks))
     tables = list(map(in_hbm, (counts, source_slot, target_owner, target_block)))
     table_shape = pltpu.VMEM((exchanges, records), jnp.int32)
     params = pltpu.CompilerParams(vmem_limit_bytes=24 * 1024 * 1024)
@@ -275,7 +294,6 @@
         pltpu.VMEM((slots, width, width), jnp.bfloat16),
         pltpu.VMEM((records, width, width), jnp.bfloat16),
     ]
-    half_shape = pltpu.VMEM((records // 2, width, width), jnp.bfloat16)
     filled_scratch = pltpu.SMEM((owners,), jnp.int32)
     table_scratch = pltpu.SMEM((exchanges, records), jnp.int32)
     level_sems = pltpu.SemaphoreType.DMA((2 + CHUNKS,))
@@ -287,12 +305,9 @@
             pltpu.VMEM(counts.shape, jnp.int32),
             table_shape,
             table_shape,
-            *acc_shapes,
-            *level_shapes[:2],
-            half_shape,
         ],
         in_specs=[HBM] * 7,
-        out_specs=[VMEM] * (8 + CHAINS),
+        out_specs=[VMEM] * 5,
         scratch_shapes=[
             *level_shapes,
             table_shape,
@@ -301,14 +316,14 @@
             filled_scratch,
             pltpu.SemaphoreType.DMA((6,)),
             level_sems,
-            level_sems,
         ],
         compiler_params=params,
         name="level_0",
-    )(*tables, right_side, diag_inverse, off_blocks)
+    )(*tables, *map(in_hbm, (right_side, diag_inverse, off_blocks)))
     solved, outgoing, counts, source_slot, target_owner = out[:5]
-    accs = out[5 : 5 + CHAINS]
-    held = out[5 + CHAINS :]
+    accs = []
+    in_vmem = lambda x: pltpu.with_memory_space_constraint(x, pltpu.VMEM)
+    held = list(map(in_vmem, (right_side, diag_inverse, off_blocks)))
     outgoing = outgoing.reshape(owners, stride, 1, width)
     arrived = lax.all_to_all(outgoing, AXES, 0, 0, tiled=True).reshape(owners * stride, width)
     results = [solved]
@@ -317,32 +332,31 @@
     for level in range(1, levels):
         last = level == levels - 1
         args = [counts, arrived, *accs]
-        specs = [VMEM] * (2 + CHAINS)
+        specs = [VMEM] * len(args)
         if level > 1:
             args += [label_table]
             specs += [VMEM]
         args += held[:2]
         specs += [VMEM] * 2
-        tail = [pltpu.SMEM(label_shape, jnp.int32)]
+        tail = [
+            pltpu.VMEM((slots * height, width), jnp.float32),
+            pltpu.SemaphoreType.REGULAR,
+        ]
         aliases = {}
         if not last:
-            more = 3 if level < levels - 2 else 2
             args += [source_slot, target_owner, held[2]]
-            args += [right_side, diag_inverse, off_blocks][:more]
-            specs += [VMEM] * 3 + [HBM] * more
+            specs += [VMEM] * 3
             shapes = [
                 solved_shape,
                 pltpu.VMEM((owners * CAP * height, width), jnp.float32),
                 *acc_shapes,
-                *level_shapes[:more],
             ]
-            aliases = {2 + chain: 2 + chain for chain in range(CHAINS)}
+            aliases = {2 + chain: 2 + chain for chain in range(len(accs))}
             if level == 1:
                 shapes += [pltpu.VMEM(label_shape, jnp.int32)]
             out_specs = [VMEM] * len(shapes)
-            scratch = [table_scratch, table_scratch, filled_scratch, level_sems] + tail
-            if level == 1:
-                scratch = [half_shape, level_sems] + scratch
+            label_scratch = pltpu.SMEM(label_shape, jnp.int32)
+            scratch = [table_scratch, table_scratch, label_scratch, filled_scratch] + tail
             scratch += [pltpu.SemaphoreType.DMA((3,))]
         else:
             args += results
@@ -365,9 +379,8 @@
             return out
         solved, outgoing = out[:2]
         accs = out[2 : 2 + CHAINS]
-        held = out[2 + CHAINS : 2 + CHAINS + more]
         if level == 1:
-            label_table = out[2 + CHAINS + more]
+            label_table = out[2 + CHAINS]
         results.append(solved)
         outgoing = outgoing.reshape(owners, CAP * height, width)
         arrived = lax.all_to_all(outgoing, AXES, 0, 0, tiled=True)

time: 116 us -> 114 us (0.983)
  Pallas kernels: 13.5 us -> 11.5 us
    pallas_call x4, Pallas kernels: 10.1 us -> 7.79 us  [shards(): pl.pallas_call(functools.partial(later_kernel, level, levels), out_shape=...]
where the time goes in v4:
time: 114 us; the launch traced here: 113 us
  blocking collectives  102 us (89%)
  Pallas kernels  11.5 us (10%)
    all_to_all x3, blocking collectives, shards(): arrived = lax.all_to_all(outgoing, AXES, 0, 0, tiled=True)  70.6 us
    all_to_all x1, blocking collectives, shards(): lax.all_to_all(outgoing, AXES, 0, 0, tiled=True)  31.2 us
    pallas_call x4, Pallas kernels, shards(): pl.pallas_call(functools.partial(later_kernel, level, levels), out_shape=...  7.79 us
    pallas_call x1, Pallas kernels, shards(): pl.pallas_call(functools.partial(first_kernel, dummy), out_shape=[solved_...  3.74 us

profile of v4, /device:TPU:1, one launch (start us, length us, event | category | flops | bytes accessed | tf_op | source)
XLA Modules:
  0.0 113.4 jit_solution(690189079381922936)
XLA Ops:
  0.0 0.0 copy-start
  0.0 0.0 copy-start.1
  0.0 0.0 copy-start.2
  0.0 3.7 %level_0.1 = (f32[16,8,128]{2,1,0:T(8,128)S(1)}, f32[2176,128]{1,0:T(8,128)S(1)}, s32[1,5]{1,0:T(1,128)S(1)}, s32[4,128]{1,0:T(4,128)S(1)}, s32[4,128]{1,0:T(4,128)S(1)}) custom-call(s32[1,5]{1,0:T(1,128)} %bitcast.17, s32[4,128]{1,0:T(4,128)} %source_hbm.1, s32[4,128]{1,0:T(4,128)} %owner_hbm.1, s32[4,128]{1,0:T(4,128)} %block_hbm.1, ...), custom_call_target="tpu_custom_call" | custom-call | tf_op jit(solution)/shard_map/level_0/pallas_call | solution.py:300
  3.8 31.2 %all_to_all.20 = f32[128,17,1,128]{3,2,1,0:T(1,128)S(1)} all-to-all(f32[128,17,1,128]{3,2,1,0:T(1,128)S(1)} %bitcast.13), channel_id=1, replica_groups=mesh['gx'=4,'gy'=4,'gz'=8] {'gx','gy','gz'}, dimensions={0} | all-to-all | bytes 2228224 | tf_op jit(solution)/shard_map/all_to_all | solution.py:328
  34.9 0.0 copy-done
  34.9 0.0 copy-done.1
  34.9 0.0 copy-done.2
  34.9 2.3 %level_1.1 = (f32[16,8,128]{2,1,0:T(8,128)S(1)}, f32[2048,128]{1,0:T(8,128)S(1)}, f32[81,8,128]{2,1,0:T(8,128)S(1)}, f32[81,8,128]{2,1,0:T(8,128)S(1)}, f32[81,8...) custom-call(s32[1,5]{1,0:T(1,128)S(1)} %get-tuple-element.29.refs_0_, f32[2176,128]{1,0:T(8,128)S(1)} %bitcast.9, ...), custom_call_target="tpu_custom_call" | custom-call | tf_op jit(solution)/shard_map/level_1/pallas_call | solution.py:368
  37.2 23.6 %all_to_all.21 = f32[128,16,128]{2,1,0:T(8,128)S(1)} all-to-all(f32[128,16,128]{2,1,0:T(8,128)S(1)} %bitcast.16), channel_id=1, replica_groups=mesh['gx'=4,'gy'=4,'gz'=8] {'gx','gy','gz'}, dimensions={0} | all-to-all | bytes 2097152 | tf_op jit(solution)/shard_map/all_to_all | solution.py:386
  60.7 2.1 %level_2.1 = (f32[16,8,128]{2,1,0:T(8,128)S(1)}, f32[2048,128]{1,0:T(8,128)S(1)}, f32[81,8,128]{2,1,0:T(8,128)S(1)}, f32[81,8,128]{2,1,0:T(8,128)S(1)}, f32[81,8...) custom-call(s32[1,5]{1,0:T(1,128)S(1)} %get-tuple-element.29.refs_0_, ...), custom_call_target="tpu_custom_call", output_to_operand_aliasing={{2}: (2, {}), {3}: (3, {}), {4}: (4, {}), {5}: (5, {})} | custom-call | tf_op jit(solution)/shard_map/level_2/pallas_call | solution.py:368
  62.8 23.5 %all_to_all.22 = f32[128,16,128]{2,1,0:T(8,128)S(1)} all-to-all(f32[128,16,128]{2,1,0:T(8,128)S(1)} %bitcast.15), channel_id=1, replica_groups=mesh['gx'=4,'gy'=4,'gz'=8] {'gx','gy','gz'}, dimensions={0} | all-to-all | bytes 2097152 | tf_op jit(solution)/shard_map/all_to_all | solution.py:386
  86.4 2.1 %level_3.1 = (f32[16,8,128]{2,1,0:T(8,128)S(1)}, f32[2048,128]{1,0:T(8,128)S(1)}, f32[81,8,128]{2,1,0:T(8,128)S(1)}, f32[81,8,128]{2,1,0:T(8,128)S(1)}, f32[81,8...) custom-call(s32[1,5]{1,0:T(1,128)S(1)} %get-tuple-element.29.refs_0_, ...), custom_call_target="tpu_custom_call", output_to_operand_aliasing={{2}: (2, {}), {3}: (3, {}), {4}: (4, {}), {5}: (5, {})} | custom-call | tf_op jit(solution)/shard_map/level_3/pallas_call | solution.py:368
  88.5 23.5 %all_to_all.23 = f32[128,16,128]{2,1,0:T(8,128)S(1)} all-to-all(f32[128,16,128]{2,1,0:T(8,128)S(1)} %bitcast.14), channel_id=1, replica_groups=mesh['gx'=4,'gy'=4,'gz'=8] {'gx','gy','gz'}, dimensions={0} | all-to-all | bytes 2097152 | tf_op jit(solution)/shard_map/all_to_all | solution.py:386
  112.0 1.3 %level_4.1 = f32[5,16,8,128]{3,2,1,0:T(8,128)} custom-call(s32[1,5]{1,0:T(1,128)S(1)} %get-tuple-element.29.refs_0_, f32[2048,128]{1,0:T(8,128)S(1)} %bitcast.12, f32[81,8,128]{2,1,0:T(8,128)S(1)} %get-tuple-element.45.refs_2_, f32[81,8,128]{2,1,0:T(8,128)S(1)} %get-tuple-element.46.refs_3_, f32[81,8,128]{2,1,0:T(8,128)S(1)} %get-tuple-element.47.refs_4_, ...), custom_call_target="tpu_custom_call" | custom-call | tf_op jit(solution)/shard_map/level_4/pallas_call | solution.py:368
Async XLA Ops:
  0.0 34.9 %copy-start = (bf16[4,128,128,128]{3,2,1,0:T(8,128)(2,1)S(1)}, bf16[4,128,128,128]{3,2,1,0:T(8,128)(2,1)}, u32[]{:S(2)}) copy-start(bf16[4,128,128,128]{3,2,1,0:T(8,128)(2,1)} %refs_11_.3) | copy-start | bytes 50331652
  0.0 34.9 %copy-start.1 = (bf16[5,16,128,128]{3,2,1,0:T(8,128)(2,1)S(1)}, bf16[5,16,128,128]{3,2,1,0:T(8,128)(2,1)}, u32[]{:S(2)}) copy-start(bf16[5,16,128,128]{3,2,1,0:T(8,128)(2,1)} %refs_8_.5) | copy-start | bytes 7864324
  0.0 34.9 %copy-start.2 = (f32[5,16,8,128]{3,2,1,0:T(8,128)S(1)}, f32[5,16,8,128]{3,2,1,0:T(8,128)}, u32[]{:S(2)}) copy-start(f32[5,16,8,128]{3,2,1,0:T(8,128)} %refs_7_.5) | copy-start | bytes 983044
